TPU v7x, 512 devices: a 4x2x32 block of a 4x8x32 slice. The times are simulated.
512 devices in a mesh: groups: 2 (over y), beam: 128 (over z, x), mp: 2 (over core).
Axes of the slice: x: 4, y: 2, z: 32, core: 2. Of those that a mesh axis runs over, the one named last changes fastest.
The devices are a block of a 4x8x32 slice.
Arguments:
- states: float32 [1024, 8, 128, 128], P(('groups', 'beam'), 'mp'), parts along dimension 0, may hold values from -4 to 4
- parent_beam: int32 [1024], P(('groups', 'beam')), parts along dimension 0, may hold values from 0 to 7, as said below
- next_token: int32 [1024], P(('groups', 'beam')), parts along dimension 0, may hold values from 0 to 16383
- proj_table: bfloat16 [16384, 8, 640], P('beam', 'mp'), may hold values from -6 to 6
- gate_table: bfloat16 [16384, 3, 8], P('beam', None, 'mp'), may hold values from -6 to 6
- gain: float32 [8, 128], P('mp'), may hold values from 0.1 to 1.9
Outputs:
- readout: bfloat16 [1024, 8, 128], P(('groups', 'beam'), 'mp'), parts along dimension 0
- new_states: float32 [1024, 8, 128, 128], P(('groups', 'beam'), 'mp'), parts along dimension 0
There are 2 independent parts, one for each index of `groups`. A program takes and returns all parts, laid end to end along the dimension named above; an argument that names none is the same for every part. Nothing has to cross between parts.
Inputs may be any that keep to these rules, and one draw needn't show every extreme that they name: The parent of hypothesis h = b * 64 + u is parent_beam[h] * 64 + u. In each aligned block of 4 hypotheses at most 2 take their parent from any one beam other than their own beam, and every block has a beam that supplies exactly 2.
All inputs are finite; a program needn't handle non-finite values.
Results may differ from a plain program's by a relative error of at most 0.001.
Values may be sent and summed in bfloat16 or wider, within the bound.
A program may use at most 64 MiB of HBM per device.

v0:
```python
import jax
import jax.numpy as jnp
from jax import lax
from jax.sharding import PartitionSpec as P

HEAD_DIM = 128
BEAMS = 8
CAP = 2


def sent_together(arrays, axis, split_dim, concat_dim, along):
    both = jnp.concatenate(arrays, axis=along)
    whole, at, outs = (
        lax.all_to_all(both, axis, split_axis=split_dim, concat_axis=concat_dim, tiled=True),
        0,
        [],
    )
    for a in arrays:
        outs.append(lax.slice_in_dim(whole, at, at + a.shape[along], axis=along))
        at += a.shape[along]
    return tuple(outs)


def from_behind(block, axis, distance):
    devices = range(lax.axis_size(axis))
    route = [((i - distance) % len(devices), i) for i in devices]
    return lax.ppermute(block, axis, route)


def unit_norm(vector):
    return vector * lax.rsqrt(jnp.sum(vector * vector, axis=-1, keepdims=True) + 1e-06)


def advance(parents, entries, gate_entries, gain):
    retain = jax.nn.sigmoid(gate_entries[:, 0, :])
    strengths = 2.0 * jax.nn.sigmoid(gate_entries[:, 1:, :])
    state_now = retain[:, :, None, None] * parents
    for reflect in range(2):
        key_unit = unit_norm(entries[:, :, 1 + reflect, :])
        value_row = entries[:, :, 3 + reflect, :]
        applied = jnp.einsum("nhvd,nhd->nhv", state_now, key_unit, precision=lax.Precision.HIGHEST)
        state_now = (
            state_now
            - strengths[:, reflect, :, None, None]
            * (applied - value_row)[:, :, :, None]
            * key_unit[:, :, None, :]
        )
    query_unit = unit_norm(entries[:, :, 0, :])
    readout = jnp.einsum("nhvd,nhd->nhv", state_now, query_unit, precision=lax.Precision.HIGHEST)
    normed = (
        gain[None, :, :]
        * readout
        * lax.rsqrt(jnp.mean(readout * readout, axis=-1, keepdims=True) + 1e-05)
    )
    return (normed.astype(jnp.bfloat16), state_now)


def local(states, parent_beam, next_token, proj_table, gate_table, gain):
    hyp_rows = states.shape[0]
    head_count = states.shape[1]
    devices = lax.axis_size("beam")
    spacing = devices // BEAMS
    position = lax.axis_index("beam")
    my_beam = position // spacing
    offset = (my_beam - parent_beam) % BEAMS
    tokens_all, parents_all = (
        lax.all_gather(next_token, "beam", axis=0, tiled=True),
        lax.all_gather(parent_beam, "beam", axis=0, tiled=True),
    )
    vocab_rows = proj_table.shape[0]
    local_ids = tokens_all - position * vocab_rows
    onehot = (local_ids[:, None] == jnp.arange(vocab_rows, dtype=jnp.int32)[None, :]).astype(
        jnp.bfloat16
    )
    flat_table = proj_table.reshape(vocab_rows, head_count * 5 * HEAD_DIM)
    flat_gates = gate_table.reshape(vocab_rows, 3 * head_count)
    looked = jnp.dot(onehot, flat_table, preferred_element_type=jnp.float32).astype(jnp.bfloat16)
    looked_gates = jnp.dot(onehot, flat_gates, preferred_element_type=jnp.float32).astype(
        jnp.bfloat16
    )
    looked = looked.reshape(devices, hyp_rows, head_count * 5 * HEAD_DIM)
    looked_gates = looked_gates.reshape(devices, hyp_rows, 3 * head_count)
    arrived, arrived_gates = sent_together((looked, looked_gates), "beam", 0, 0, 2)
    entries = jnp.sum(arrived, axis=0, dtype=jnp.float32).reshape(hyp_rows, head_count, 5, HEAD_DIM)
    gate_entries = jnp.sum(arrived_gates, axis=0, dtype=jnp.float32).reshape(
        hyp_rows, 3, head_count
    )
    parents = jnp.where((offset == 0)[:, None, None, None], states, jnp.zeros_like(states))
    slot_ids = jnp.arange(CAP, dtype=jnp.int32)
    for distance in range(1, BEAMS):
        target = (position + distance * spacing) % devices
        their_parents = lax.dynamic_slice_in_dim(parents_all, target * hyp_rows, hyp_rows)
        needed = their_parents == my_beam
        slot_rank = jnp.cumsum(needed.astype(jnp.int32)) - 1
        select = ((slot_rank[None, :] == slot_ids[:, None]) & needed[None, :]).astype(jnp.float32)
        packed = jnp.einsum("cr,rhij->chij", select, states, precision=lax.Precision.HIGHEST)
        received = from_behind(packed, "beam", distance * spacing)
        wanted = offset == distance
        wanted_rank = jnp.cumsum(wanted.astype(jnp.int32)) - 1
        placing = ((wanted_rank[:, None] == slot_ids[None, :]) & wanted[:, None]).astype(
            jnp.float32
        )
        parents = parents + jnp.einsum(
            "rc,chij->rhij", placing, received, precision=lax.Precision.HIGHEST
        )
    return advance(parents, entries, gate_entries, gain)


def solution(mesh):
    return jax.shard_map(
        local,
        mesh=mesh,
        in_specs=(
            P(("groups", "beam"), "mp", None, None),
            P(("groups", "beam")),
            P(("groups", "beam")),
            P("beam", "mp", None),
            P("beam", None, "mp"),
            P("mp", None),
        ),
        out_specs=(P(("groups", "beam"), "mp", None), P(("groups", "beam"), "mp", None, None)),
        check_vma=False,
    )
```

profile of v0, /device:TPU:108, one launch (start us, length us, event | category | flops | bytes accessed | tf_op | source)
XLA Modules:
  0.0 742.2 jit_solution(130754689765989549)
XLA Ops:
  5.0 74.3 %all-reduce.2 = (s32[512]{0:T(512)S(1)}, s32[512]{0:T(512)S(1)}) all-reduce(s32[512]{0:T(512)S(1)} %dynamic-update-slice.1, s32[512]{0:T(512)S(1)} %dynamic-update-slice), channel_id=1, replica_groups=mesh['groups'=2,'beam'=128,'mp'=2] {'beam'}, use_global_device_ids=true, to_apply=%add.1 | all-reduce | flops 1024 | bytes 8192
  80.8 2.4 convolution_convert_fusion
  83.2 5.5 reshape.461
  88.8 4.6 pad_maximum_fusion
  93.3 12.6 %all-to-all-start = ((bf16[128,4,2572]{2,1,0:T(4,128)(2,1)}), bf16[128,4,2572]{2,1,0:T(4,128)(2,1)}, u32[]{:S(2)}, u32[]{:S(2)}) async-start(bf16[128,4,2572]{2,1,0:T(4,128)(2,1)} %pad_maximum_fusion), calls=%async_computation | async-start | bytes 5505024 | tf_op jit(solution)/shard_map/all_to_all | solution.py:14
  108.0 8.6 %collective-permute-start.6 = (f32[2,4,128,128]{3,0,2,1:T(2,128)S(1)}, f32[2,4,128,128]{3,0,2,1:T(2,128)S(1)}, u32[]{:S(2)}, u32[]{:S(2)}) collective-permute-start(f32[2,4,128,128]{3,0,2,1:T(2,128)S(1)} %fusion.11), channel_id=1, source_target_pairs={{32,0},{34,2},{36,4},{38,6},{40,8},{42,10},{44,12},{46,14},{48,16}... | collective-permute-start | bytes 1572872 | tf_op jit(solution)/shard_map/ppermute | solution.py:27
  116.8 2.5 fusion.13
  119.2 11.8 %collective-permute-start.5 = (f32[2,4,128,128]{3,0,2,1:T(2,128)}, f32[2,4,128,128]{3,0,2,1:T(2,128)S(1)}, u32[]{:S(2)}, u32[]{:S(2)}) collective-permute-start(f32[2,4,128,128]{3,0,2,1:T(2,128)} %fusion.13), channel_id=1, source_target_pairs={{64,0},{66,2},{68,4},{70,6},{72,8},{74,10},{76,12},{78,14},{80,16}... | collective-permute-start | bytes 1572872 | tf_op jit(solution)/shard_map/ppermute | solution.py:27
  131.2 2.5 fusion.15
  133.7 7.3 collective-permute-start.4
  141.1 2.5 fusion.17
  143.6 12.5 %collective-permute-start.3 = (f32[2,4,128,128]{3,0,2,1:T(2,128)}, f32[2,4,128,128]{3,0,2,1:T(2,128)}, u32[]{:S(2)}, u32[]{:S(2)}) collective-permute-start(f32[2,4,128,128]{3,0,2,1:T(2,128)} %fusion.17), channel_id=1, source_target_pairs={{128,0},{130,2},{132,4},{134,6},{136,8},{138,10},{140,12},{142,14}... | collective-permute-start | bytes 1572872 | tf_op jit(solution)/shard_map/ppermute | solution.py:27
  156.2 2.5 fusion.19
  158.7 6.7 collective-permute-start.2
  167.1 1.7 fusion.21
  168.8 2.5 fusion.23
  171.2 237.7 %collective-permute-done.6 = f32[2,4,128,128]{3,0,2,1:T(2,128)S(1)} collective-permute-done((f32[2,4,128,128]{3,0,2,1:T(2,128)S(1)}, f32[2,4,128,128]{3,0,2,1:T(2,128)S(1)}, u32[]{:S(2)}, u32[]{:S(2)}) %collective-permute-start.6) | collective-permute-done | bytes 524320 | tf_op jit(solution)/shard_map/ppermute | solution.py:27
  408.9 11.6 %collective-permute-start.1 = (f32[2,4,128,128]{3,0,2,1:T(2,128)S(1)}, f32[2,4,128,128]{3,0,2,1:T(2,128)S(1)}, u32[]{:S(2)}, u32[]{:S(2)}) collective-permute-start(f32[2,4,128,128]{3,0,2,1:T(2,128)S(1)} %fusion.21), channel_id=1, source_target_pairs={{192,0},{194,2},{196,4},{198,6},{200,8},{202,10},{204,12},{206,14}... | collective-permute-start | bytes 1572872 | tf_op jit(solution)/shard_map/ppermute | solution.py:27
  421.8 107.7 %collective-permute-done.5 = f32[2,4,128,128]{3,0,2,1:T(2,128)S(1)} collective-permute-done((f32[2,4,128,128]{3,0,2,1:T(2,128)}, f32[2,4,128,128]{3,0,2,1:T(2,128)S(1)}, u32[]{:S(2)}, u32[]{:S(2)}) %collective-permute-start.5) | collective-permute-done | bytes 524320 | tf_op jit(solution)/shard_map/ppermute | solution.py:27
  529.6 6.5 collective-permute-start
  536.1 2.3 fusion.38
  538.3 116.9 %collective-permute-done.4 = f32[2,4,128,128]{3,0,2,1:T(2,128)} collective-permute-done((f32[2,4,128,128]{3,0,2,1:T(2,128)}, f32[2,4,128,128]{3,0,2,1:T(2,128)}, u32[]{:S(2)}, u32[]{:S(2)}) %collective-permute-start.4) | collective-permute-done | bytes 524320 | tf_op jit(solution)/shard_map/ppermute | solution.py:27
  655.2 3.3 fusion.41
  658.6 55.3 %collective-permute-done.3 = f32[2,4,128,128]{3,0,2,1:T(2,128)} collective-permute-done((f32[2,4,128,128]{3,0,2,1:T(2,128)}, f32[2,4,128,128]{3,0,2,1:T(2,128)}, u32[]{:S(2)}, u32[]{:S(2)}) %collective-permute-start.3) | collective-permute-done | bytes 524320 | tf_op jit(solution)/shard_map/ppermute | solution.py:27
  713.9 3.3 fusion.44
  717.2 3.4 fusion.47
  720.6 2.4 fusion.50
  724.1 2.8 convert_reduce_fusion
  728.4 4.5 fusion.6
  732.9 1.7 fusion.9
  735.6 1.7 fusion.7
  739.2 1.7 fusion.128
  (86 shorter events, 17.0 us)
Async XLA Ops:
  93.3 13.0 %copy-start = (f32[4,4,128,128]{3,2,1,0:T(8,128)S(1)}, f32[4,4,128,128]{3,2,1,0:T(8,128)}, u32[]{:S(2)}) copy-start(f32[4,4,128,128]{3,2,1,0:T(8,128)} %param.6) | copy-start | bytes 3145732
  93.3 629.6 %all-to-all-start = ((bf16[128,4,2572]{2,1,0:T(4,128)(2,1)}), bf16[128,4,2572]{2,1,0:T(4,128)(2,1)}, u32[]{:S(2)}, u32[]{:S(2)}) async-start(bf16[128,4,2572]{2,1,0:T(4,128)(2,1)} %pad_maximum_fusion), calls=%async_computation | async-start | bytes 5505024 | tf_op jit(solution)/shard_map/all_to_all | solution.py:14
  108.0 300.9 %collective-permute-start.6 = (f32[2,4,128,128]{3,0,2,1:T(2,128)S(1)}, f32[2,4,128,128]{3,0,2,1:T(2,128)S(1)}, u32[]{:S(2)}, u32[]{:S(2)}) collective-permute-start(f32[2,4,128,128]{3,0,2,1:T(2,128)S(1)} %fusion.11), channel_id=1, source_target_pairs={{32,0},{34,2},{36,4},{38,6},{40,8},{42,10},{44,12},{46,14},{48,16}... | collective-permute-start | bytes 1572872 | tf_op jit(solution)/shard_map/ppermute | solution.py:27
  119.2 46.2 %copy-start.4 = (s32[4]{0:T(128)S(1)}, s32[4]{0:T(128)}, u32[]{:S(2)}) copy-start(s32[4]{0:T(128)} %param.7) | copy-start | bytes 52
  119.2 410.4 %collective-permute-start.5 = (f32[2,4,128,128]{3,0,2,1:T(2,128)}, f32[2,4,128,128]{3,0,2,1:T(2,128)S(1)}, u32[]{:S(2)}, u32[]{:S(2)}) collective-permute-start(f32[2,4,128,128]{3,0,2,1:T(2,128)} %fusion.13), channel_id=1, source_target_pairs={{64,0},{66,2},{68,4},{70,6},{72,8},{74,10},{76,12},{78,14},{80,16}... | collective-permute-start | bytes 1572872 | tf_op jit(solution)/shard_map/ppermute | solution.py:27
  133.7 521.6 %collective-permute-start.4 = (f32[2,4,128,128]{3,0,2,1:T(2,128)}, f32[2,4,128,128]{3,0,2,1:T(2,128)}, u32[]{:S(2)}, u32[]{:S(2)}) collective-permute-start(f32[2,4,128,128]{3,0,2,1:T(2,128)} %fusion.15), channel_id=1, source_target_pairs={{96,0},{98,2},{100,4},{102,6},{104,8},{106,10},{108,12},{110,14},{... | collective-permute-start | bytes 1572872 | tf_op jit(solution)/shard_map/ppermute | solution.py:27
  143.6 570.3 %collective-permute-start.3 = (f32[2,4,128,128]{3,0,2,1:T(2,128)}, f32[2,4,128,128]{3,0,2,1:T(2,128)}, u32[]{:S(2)}, u32[]{:S(2)}) collective-permute-start(f32[2,4,128,128]{3,0,2,1:T(2,128)} %fusion.17), channel_id=1, source_target_pairs={{128,0},{130,2},{132,4},{134,6},{136,8},{138,10},{140,12},{142,14}... | collective-permute-start | bytes 1572872 | tf_op jit(solution)/shard_map/ppermute | solution.py:27
  158.7 558.5 %collective-permute-start.2 = (f32[2,4,128,128]{3,0,2,1:T(2,128)}, f32[2,4,128,128]{3,0,2,1:T(2,128)}, u32[]{:S(2)}, u32[]{:S(2)}) collective-permute-start(f32[2,4,128,128]{3,0,2,1:T(2,128)} %fusion.19), channel_id=1, source_target_pairs={{160,0},{162,2},{164,4},{166,6},{168,8},{170,10},{172,12},{174,14}... | collective-permute-start | bytes 1572872 | tf_op jit(solution)/shard_map/ppermute | solution.py:27
  408.9 311.7 %collective-permute-start.1 = (f32[2,4,128,128]{3,0,2,1:T(2,128)S(1)}, f32[2,4,128,128]{3,0,2,1:T(2,128)S(1)}, u32[]{:S(2)}, u32[]{:S(2)}) collective-permute-start(f32[2,4,128,128]{3,0,2,1:T(2,128)S(1)} %fusion.21), channel_id=1, source_target_pairs={{192,0},{194,2},{196,4},{198,6},{200,8},{202,10},{204,12},{206,14}... | collective-permute-start | bytes 1572872 | tf_op jit(solution)/shard_map/ppermute | solution.py:27
  529.6 198.0 %collective-permute-start = (f32[2,4,128,128]{3,0,2,1:T(2,128)}, f32[2,4,128,128]{3,0,2,1:T(2,128)S(1)}, u32[]{:S(2)}, u32[]{:S(2)}) collective-permute-start(f32[2,4,128,128]{3,0,2,1:T(2,128)} %fusion.23), channel_id=1, source_target_pairs={{224,0},{226,2},{228,4},{230,6},{232,8},{234,10},{236,12},{238,14}... | collective-permute-start | bytes 1572872 | tf_op jit(solution)/shard_map/ppermute | solution.py:27
  727.6 0.8 copy-start.2
  737.5 3.5 copy-start.3
  739.0 2.7 copy-start.1
where the time goes:
time: 751 us; the launch traced here: 742 us
  waiting for transfers between devices  518 us (69%)
  starting transfers between devices  77.5 us (10%)
  blocking collectives  74.3 us (10%)
  matrix products  43.9 us (6%)
  other arithmetic  14.8 us (2%)
  local copies, waits for them, and re-layouts  12 us (2%)
    ppermute x7, waiting for transfers between devices, from_behind(): return lax.ppermute(block, axis, route)  518 us
    unnamed x1, blocking collectives  74.3 us
    ppermute x7, starting transfers between devices, from_behind(): return lax.ppermute(block, axis, route)  64.9 us
    dot_general x7, matrix products, local(): jnp.einsum('rc,chij->rhij', placing, received, precision=lax.Precision.HI...  20.5 us
    dot_general x7, matrix products, local(): jnp.einsum('cr,rhij->chij', select, states, precision=lax.Precision.HIGHEST)  15.6 us
  transfers between devices with their start and end apart: 8, of which 4 were waited for; matrix products, arithmetic and copies ran while one was open for 5% of the time, Pallas kernels for 0%

commit v1 on v0

v1 whole, which is shorter than its diff:
```python
import functools

import jax
import jax.numpy as jnp
from jax import lax
from jax.experimental import pallas as pl
from jax.experimental.pallas import tpu as pltpu
from jax.sharding import PartitionSpec as P

BEAMS = 8
ROW = 4
IDS = 8
LEVELS = 32767.0


def to(index):
    return dict(device_id={"beam": index}, device_id_type=pl.DeviceIdType.MESH)


def gather_kernel(count, states, ids, items, scales, table, q, qs, near, side, tile, sems, rsem):
    n = lax.axis_size("beam")
    me = lax.axis_index("beam")
    spacing = n // BEAMS
    rows = spacing // ROW
    my_beam, within = me // spacing, me % spacing
    row, col = within // ROW, within % ROW
    base = my_beam * spacing
    beam_peers = [(me + k * spacing) % n for k in range(1, BEAMS)]
    row_peers = [base + ((row + k) % rows) * ROW + col for k in range(1, rows)]
    col_peers = [base + row * ROW + (col + k) % ROW for k in range(1, ROW)]
    peers = beam_peers + row_peers + col_peers
    barrier = pltpu.get_barrier_semaphore()
    for p in peers:
        pl.semaphore_signal(barrier, inc=1, **to(p))
    pl.semaphore_wait(barrier, len(peers))

    copies = []
    at = [0]

    def send(src, dst, target):
        c = pltpu.make_async_remote_copy(
            src_ref=src, dst_ref=dst, send_sem=sems.at[at[0]], recv_sem=rsem.at[at[0]], **to(target)
        )
        at[0] += 1
        c.start()
        copies.append(c)
        return c

    def code(u):
        for h in range(states.shape[1]):
            x = states[u, h]
            top = jnp.maximum(jnp.max(jnp.abs(x), axis=0, keepdims=True), 1e-30)
            qs[u, h : h + 1, :] = top * (1.0 / LEVELS)
            q[u, h] = lax.round(
                x * (LEVELS / top), lax.RoundingMethod.TO_NEAREST_EVEN
            ).astype(jnp.int32).astype(jnp.int16)

    first = [send(ids, near.at[k], p) for k, p in enumerate(row_peers)]
    code(0)
    ways = (beam_peers[0], beam_peers[-1])
    for d in range(2):
        send(q.at[0], items.at[d * count], ways[d])
    for c in first:
        c.wait_recv()
    total = ids[...]
    for k in range(len(row_peers)):
        total = total + near[k]
    tile[0] = total
    for u in range(1, count):
        code(u)
    second = [send(tile.at[0], side.at[k], p) for k, p in enumerate(col_peers)]
    for c in second:
        c.wait_recv()
    for k in range(len(col_peers)):
        total = total + side[k]
    tile[1] = total
    for d in range(2):
        send(qs, scales.at[d], ways[d])
    for k, p in enumerate(beam_peers):
        send(tile.at[1], table.at[k + 1], p)
    for u in range(1, count):
        for d in range(2):
            send(q.at[u], items.at[d * count + u], ways[d])
    table[0] = total
    waited = set(map(id, first + second))
    for c in copies:
        c.wait_send()
        if id(c) not in waited:
            c.wait_recv()


def gather(states, ids):
    count, heads, size, _ = states.shape
    n = lax.axis_size("beam")
    rows = n // BEAMS // ROW
    sends = (rows - 1) + (ROW - 1) + (BEAMS - 1) + 2 * count + 2
    whole = pl.BlockSpec(memory_space=pltpu.VMEM)
    return pl.pallas_call(
        functools.partial(gather_kernel, count),
        out_shape=(
            jax.ShapeDtypeStruct((2 * count, heads, size, size), jnp.int16),
            jax.ShapeDtypeStruct((2, count, heads, size), jnp.float32),
            jax.ShapeDtypeStruct((BEAMS, 8, 128), jnp.int32),
        ),
        in_specs=[whole, whole],
        out_specs=(whole, whole, whole),
        scratch_shapes=[
            pltpu.VMEM((count, heads, size, size), jnp.int16),
            pltpu.VMEM((count, heads, size), jnp.float32),
            pltpu.VMEM((rows - 1, 8, 128), jnp.int32),
            pltpu.VMEM((ROW - 1, 8, 128), jnp.int32),
            pltpu.VMEM((2, 8, 128), jnp.int32),
            pltpu.SemaphoreType.DMA((sends,)),
            pltpu.SemaphoreType.DMA((sends,)),
        ],
        compiler_params=pltpu.CompilerParams(
            collective_id=0, has_side_effects=True, vmem_limit_bytes=24 << 20
        ),
    )(states, ids)


def lowest(row_of, beam, count):
    u = count - 1
    for k in range(count - 2, -1, -1):
        u = jnp.where(row_of(k) == beam, k, u)
    return u


def highest(row_of, beam, count):
    u = 0
    for k in range(1, count):
        u = jnp.where(row_of(k) == beam, k, u)
    return u


def relay_kernel(count, wants, states, items1, scales1, parents, *scratch):
    two, three, four, picked = scratch[0:2], scratch[2:4], scratch[4:6], scratch[6:8]
    two_s, three_s, four_s, picked_s = scratch[8:10], scratch[10:12], scratch[12:14], scratch[14:16]
    sems, rsem = scratch[16:]
    n = lax.axis_size("beam")
    me = lax.axis_index("beam")
    spacing = n // BEAMS
    my_beam = me // spacing
    ways = ((me + spacing) % n, (me + n - spacing) % n)
    barrier = pltpu.get_barrier_semaphore()
    for p in ways:
        pl.semaphore_signal(barrier, inc=1, **to(p))
    pl.semaphore_wait(barrier, 2)

    def beam(d):
        return (my_beam + BEAMS + d) % BEAMS

    def wanted_by(d):
        return lambda u: wants[(BEAMS - d) % BEAMS, u]

    copies = []
    at = [0]

    def send(src, dst, way):
        c = pltpu.make_async_remote_copy(
            src_ref=src, dst_ref=dst, send_sem=sems.at[at[0]], recv_sem=rsem.at[at[0]], **to(ways[way])
        )
        at[0] += 1
        c.start()
        copies.append(c)
        return c

    step2 = [[send(scales1.at[d], two_s[d], d)] for d in range(2)]
    for u in range(count):
        for d in range(2):
            step2[d].append(send(items1.at[d * count + u], two[d].at[u], d))
    step3 = []
    for d in range(2):
        for c in step2[d]:
            c.wait_recv()
        sign = 1 if d == 0 else -1
        origin = beam(-2 * sign)
        nearer = wanted_by(sign)
        farther = wanted_by(2 * sign)
        end = lowest if d == 0 else highest
        chosen = (
            lowest(nearer, origin, count), highest(nearer, origin, count), end(farther, origin, count)
        )
        for s, u in enumerate(chosen):
            picked_s[d][s] = two_s[d][u]
            picked[d][s] = two[d][u]
        step3.append([send(picked_s[d], three_s[d], d)])
        for s in (2, 0, 1):
            step3[d].append(send(picked[d].at[s], three[d].at[s], d))
    step4 = []
    for d in range(2):
        step3[d][0].wait_recv()
        step4.append(send(three_s[d].at[2], four_s[d].at[0], d))
        step3[d][1].wait_recv()
        step4.append(send(three[d].at[2], four[d].at[0], d))
    for d in range(2):
        for c in step3[d][2:]:
            c.wait_recv()
    for c in step4:
        c.wait_recv()
    mine = wanted_by(0)
    for u in range(count):
        offset = (my_beam + BEAMS - mine(u)) % BEAMS
        third = [jnp.where(lowest(mine, beam(d), count) == u, 0, 1) for d in (-3, 3)]
        middle = lowest(mine, beam(4), count) == u
        one = jnp.where(offset == BEAMS - 1, count + u, u)
        for h in range(states.shape[1]):
            x = states[u, h]

            def take(x, when, code, scale):
                return jnp.where(when, code.astype(jnp.int32).astype(jnp.float32) * scale, x)

            x = take(
                x, (offset == 1) | (offset == BEAMS - 1),
                items1[one, h], scales1[one // count, u, h : h + 1, :],
            )
            for d in range(2):
                x = take(
                    x, offset == (2, BEAMS - 2)[d], two[d][u, h], two_s[d][u, h : h + 1, :]
                )
                x = take(
                    x, offset == (3, BEAMS - 3)[d],
                    three[d][third[d], h], three_s[d][third[d], h : h + 1, :],
                )
                x = take(
                    x, (offset == 4) & (middle if d == 0 else jnp.logical_not(middle)),
                    four[d][0, h], four_s[d][0, h : h + 1, :],
                )
            parents[u, h] = x
    for c in copies:
        c.wait_send()


def relay(wants, states, items1, scales1):
    count, heads, size, _ = states.shape
    sends = 2 * (1 + count) + 2 * 4 + 4
    whole = pl.BlockSpec(memory_space=pltpu.VMEM)
    kept = [count, count, 3, 3, 1, 1, 3, 3]
    return pl.pallas_call(
        functools.partial(relay_kernel, count),
        out_shape=jax.ShapeDtypeStruct(states.shape, jnp.float32),
        in_specs=[pl.BlockSpec(memory_space=pltpu.SMEM), whole, whole, whole],
        out_specs=whole,
        scratch_shapes=[
            *(pltpu.VMEM((k, heads, size, size), jnp.int16) for k in kept),
            *(pltpu.VMEM((k, heads, size), jnp.float32) for k in kept),
            pltpu.SemaphoreType.DMA((sends,)),
            pltpu.SemaphoreType.DMA((sends,)),
        ],
        cost_estimate=pl.CostEstimate(flops=10**9, bytes_accessed=6 << 20, transcendentals=0),
        compiler_params=pltpu.CompilerParams(
            collective_id=1, has_side_effects=True, vmem_limit_bytes=24 << 20
        ),
    )(wants, states, items1, scales1)


def advance_kernel(parents, entries, gates, gain, readout, new_states):
    heads, size = parents.shape[1], parents.shape[2]
    eye = (
        lax.broadcasted_iota(jnp.int32, (size, size), 0)
        == lax.broadcasted_iota(jnp.int32, (size, size), 1)
    ).astype(jnp.float32)
    gate = jax.nn.sigmoid(gates[0])
    rows = []
    for h in range(heads):

        def entry(k):
            return entries[0, h * 5 + k : h * 5 + k + 1, :]

        def unit(x):
            return x * lax.rsqrt(jnp.sum(x * x, axis=-1, keepdims=True) + 1e-06)

        def level(k):
            return gate[k * heads + h : k * heads + h + 1, :]

        state = level(0) * parents[0, h]
        for j in range(2):
            key = unit(entry(1 + j))
            gap = jnp.sum(state * key - eye * entry(3 + j), axis=-1, keepdims=True)
            state = state - gap * (2.0 * level(1 + j) * key)
        new_states[0, h] = state
        out = jnp.sum(state * unit(entry(0)), axis=-1, keepdims=True)
        row = jnp.sum(eye * out, axis=0, keepdims=True)
        scale = lax.rsqrt(jnp.sum(row * row, axis=-1, keepdims=True) * (1.0 / size) + 1e-05)
        rows.append(gain[h : h + 1, :] * row * scale)
    readout[0] = jnp.concatenate(rows, axis=0).astype(jnp.bfloat16)


def advance(parents, entries, gates, gain):
    count, heads, size, _ = parents.shape
    return pl.pallas_call(
        advance_kernel,
        grid=(count,),
        out_shape=(
            jax.ShapeDtypeStruct((count, heads, size), jnp.bfloat16),
            jax.ShapeDtypeStruct(parents.shape, jnp.float32),
        ),
        in_specs=[
            pl.BlockSpec((1, heads, size, size), lambda i: (i, 0, 0, 0)),
            pl.BlockSpec((1, heads * 5, size), lambda i: (i, 0, 0)),
            pl.BlockSpec((1, 3 * heads, size), lambda i: (i, 0, 0)),
            pl.BlockSpec((heads, size), lambda i: (0, 0)),
        ],
        out_specs=(
            pl.BlockSpec((1, heads, size), lambda i: (i, 0, 0)),
            pl.BlockSpec((1, heads, size, size), lambda i: (i, 0, 0, 0)),
        ),
    )(parents, entries, gates, gain)


def local(states, parent_beam, next_token, proj_table, gate_table, gain):
    count, heads, size, _ = states.shape
    devices = lax.axis_size("beam")
    spacing = devices // BEAMS
    position = lax.axis_index("beam")
    my_beam, within = position // spacing, position % spacing
    lanes = jnp.zeros((128,), jnp.int32)
    mine = jnp.concatenate([next_token, parent_beam])
    lanes = lax.dynamic_update_slice(lanes, mine, (within * 2 * count,))
    ids = jnp.broadcast_to(lanes[None, :], (8, 128))
    items1, scales1, table = gather(states, ids)
    every = table[:, 0, :].reshape(BEAMS, spacing, 2 * count)
    wants = lax.dynamic_slice_in_dim(every, within, 1, axis=1)[:, 0, count:]
    order = (my_beam + BEAMS - jnp.arange(BEAMS)) % BEAMS
    tokens = jnp.take(every[:, :, :count], order, axis=0).reshape(-1)

    vocab_rows = proj_table.shape[0]
    wide = 5 * size
    padded = jnp.concatenate(
        [
            proj_table.transpose(1, 0, 2),
            gate_table.transpose(2, 0, 1),
            jnp.zeros((heads, vocab_rows, size - 3), proj_table.dtype),
        ],
        axis=2,
    ).reshape(heads * vocab_rows, wide + size)
    wanted = jnp.repeat(tokens - position * vocab_rows, heads)
    head_at = jnp.arange(heads * vocab_rows, dtype=jnp.int32) // vocab_rows
    row_at = jnp.arange(heads * vocab_rows, dtype=jnp.int32) % vocab_rows
    own_head = jnp.arange(wanted.shape[0], dtype=jnp.int32) % heads
    onehot = (
        (wanted[:, None] == row_at[None, :]) & (own_head[:, None] == head_at[None, :])
    ).astype(jnp.bfloat16)
    looked = jnp.dot(onehot, padded, preferred_element_type=jnp.float32).astype(jnp.bfloat16)
    arrived = lax.psum_scatter(looked, "beam", scatter_dimension=0, tiled=True)
    parents = relay(wants, states, items1, scales1)
    arrived = arrived.astype(jnp.float32).reshape(count, heads, wide + size)
    entries = arrived[:, :, :wide].reshape(count, heads * 5, size)
    gates = arrived[:, :, wide : wide + 3].transpose(0, 2, 1).reshape(count, 3 * heads)
    gates = jnp.broadcast_to(gates[:, :, None], (count, 3 * heads, size))
    return advance(parents, entries, gates, gain)


def solution(mesh):
    return jax.shard_map(
        local,
        mesh=mesh,
        in_specs=(
            P(("groups", "beam"), "mp", None, None),
            P(("groups", "beam")),
            P(("groups", "beam")),
            P("beam", "mp", None),
            P("beam", None, "mp"),
            P("mp", None),
        ),
        out_specs=(P(("groups", "beam"), "mp", None), P(("groups", "beam"), "mp", None, None)),
        check_vma=False,
    )
```

time: 751 us -> 2650 us (3.53)
  the two profiles are of different devices: /device:TPU:108 before, /device:TPU:40 now
where the time goes in v1:
time: 2650 us
  waiting for transfers between devices  2420 us (91%)
  Pallas kernels  200 us (8%)
    reduce_scatter x1, waiting for transfers between devices, local(): arrived = lax.psum_scatter(looked, 'beam', scatter_dimension=0, tiled=True)  2420 us
    pallas_call x1, Pallas kernels, gather(): pl.pallas_call(functools.partial(gather_kernel, count), out_shape=(jax.Sh...  102 us
    pallas_call x1, Pallas kernels, relay(): pl.pallas_call(functools.partial(relay_kernel, count), out_shape=jax.Shap...  93.4 us
  transfers between devices with their start and end apart: 1, of which 1 were waited for; matrix products, arithmetic and copies ran while one was open for 0% of the time, Pallas kernels for 4%

profile of v1, /device:TPU:40, one launch (start us, length us, event | category | flops | bytes accessed | tf_op | source)
XLA Modules:
  0.0 2651.5 jit_solution(2810971567431942015)
XLA Ops:
  7.2 0.1 reduce-scatter.2.cloned.1.call-start
  7.3 0.9 copy.15
  8.2 1.2 copy.20
  9.4 0.8 add_dynamic-update-slice_fusion
  10.2 0.0 copy-start
  10.3 1.2 copy-done
  11.5 102.1 %shard_map.77 = (s16[8,4,128,128]{3,2,1,0:T(8,128)(2,1)S(1)}, f32[2,4,4,128]{3,2,1,0:T(4,128)S(1)}, s32[8,8,128]{2,1,0:T(8,128)S(1)}) custom-call(f32[4,4,128,128]{3,2,1,0:T(8,128)S(1)} %copy-done, s32[8,128]{1,0:T(8,128)S(1)} %broadcast_in_dim.36.ids), custom_call_target="tpu_custom_call" | custom-call | tf_op jit(solution)/shard_map/pallas_call | solution.py:98
  113.6 0.1 reshape_squeeze.3
  113.7 0.6 gather_fusion
  114.2 0.1 select_subtract_fusion
  114.3 0.1 sub.45
  114.4 0.1 broadcast_in_dim.39
  114.6 0.2 eq.36
  114.7 0.1 pad.2.clone
  114.8 0.1 maximum_maximum_fusion
  115.0 3.6 fusion.4
  118.5 0.0 copy-start.1
  118.5 0.1 reduce-scatter.2.cloned.1.call-update
  118.6 0.1 constant_dynamic-slice_fusion
  118.7 1.1 copy-done.1
  119.8 93.4 %shard_map.78.parents = f32[4,4,128,128]{3,2,1,0:T(8,128)S(1)} custom-call(s32[8,4]{1,0:T(8,128)S(1)} %bitcast.11, f32[4,4,128,128]{3,2,1,0:T(8,128)S(1)} %copy-done.1, s16[8,4,128,128]{3,2,1,0:T(8,128)(2,1)S(1)} %get-tuple-element.6.items1, f32[2,4,4,128]{3,2,1,0:T(4,128)S(1)} %get-tuple-element.7.scales1), custom_call_target="tpu_custom_call" | custom-call | flops 1000000000 | bytes 6291456 | tf_op jit(solution)/shard_map/pallas_call | solution.py:239
  213.2 0.0 copy-start.2
  213.2 1.0 copy-done.2
  214.2 2424.1 %reduce-scatter.2.cloned.1.call-done = bf16[16,768]{1,0:T(8,128)(2,1)} async-done(((bf16[2048,768]{1,0:T(8,128)(2,1)}), bf16[16,768]{1,0:T(8,128)(2,1)}) %reduce-scatter.2.cloned.1.call-update) | async-done | bytes 24592 | tf_op jit(solution)/shard_map/reduce_scatter | solution.py:345
  2638.3 0.8 reshape.120
  2639.1 0.1 copy.18
  2639.2 0.1 broadcast_in_dim.41
  2639.3 0.6 reshape.118.entries
  2639.9 0.7 broadcast_in_dim.42.gates
  2640.6 4.1 shard_map.79
  (11 shorter events, 0.1 us)
Async XLA Ops:
  7.2 2631.1 %reduce-scatter.2.cloned.1.call-start = ((), (), s32[]{:S(2)}) async-start(), calls=%async_computation.1 | async-start | bytes 3170304 | tf_op jit(solution)/shard_map/reduce_scatter | solution.py:345
  10.2 1.2 copy-start
  118.5 1.2 copy-start.1
  213.2 1.0 copy-start.2
Sparse Core Ops, SparseCore 0:
  118.7 2519.5 reduce-scatter.1

commit v2 on v1

--- a/solution.py
+++ b/solution.py
@@ -133,19 +133,31 @@
     return u
 
 
-def relay_kernel(count, wants, states, items1, scales1, parents, *scratch):
+def relay_kernel(count, wants, states, items1, scales1, looked, parents, arrived, *scratch):
     two, three, four, picked = scratch[0:2], scratch[2:4], scratch[4:6], scratch[6:8]
     two_s, three_s, four_s, picked_s = scratch[8:10], scratch[10:12], scratch[12:14], scratch[14:16]
-    sems, rsem = scratch[16:]
+    opposite_half, from_cols, from_rows = scratch[16:18], scratch[18:20], scratch[20:-10]
+    part_sum, hops, from_beam = scratch[-10:-8], scratch[-8:-6], scratch[-6:-4]
+    col_sum, row_sum, sems, rsem = scratch[-4:]
     n = lax.axis_size("beam")
     me = lax.axis_index("beam")
     spacing = n // BEAMS
     my_beam = me // spacing
+    rows = spacing // ROW
+    within = me % spacing
+    row, col = within // ROW, within % ROW
+    base = my_beam * spacing
     ways = ((me + spacing) % n, (me + n - spacing) % n)
+    cols = ((col + 1) % ROW, (col + ROW - 1) % ROW)
+    across = (col + 2) % ROW
+    col_ways = [base + row * ROW + c for c in cols]
+    row_ids = [(row + k) % rows for k in range(1, rows)]
+    row_peers = [base + r * ROW + col for r in row_ids]
     barrier = pltpu.get_barrier_semaphore()
-    for p in ways:
+    peers = [*ways, *col_ways, *row_peers]
+    for p in peers:
         pl.semaphore_signal(barrier, inc=1, **to(p))
-    pl.semaphore_wait(barrier, 2)
+    pl.semaphore_wait(barrier, len(peers))
 
     def beam(d):
         return (my_beam + BEAMS + d) % BEAMS
@@ -156,20 +168,58 @@
     copies = []
     at = [0]
 
-    def send(src, dst, way):
+    def send_to(src, dst, target):
         c = pltpu.make_async_remote_copy(
-            src_ref=src, dst_ref=dst, send_sem=sems.at[at[0]], recv_sem=rsem.at[at[0]], **to(ways[way])
+            src_ref=src, dst_ref=dst, send_sem=sems.at[at[0]], recv_sem=rsem.at[at[0]], **to(target)
         )
         at[0] += 1
         c.start()
         copies.append(c)
         return c
 
+    def send(src, dst, way):
+        return send_to(src, dst, ways[way])
+
+    def add(dst, *srcs):
+        def step(i, _):
+            x = srcs[0][i]
+            for y in srcs[1:]:
+                x = x + y[i]
+            dst[i] = x
+            return 0
+
+        lax.fori_loop(0, dst.shape[0], step, 0)
+
+    blocks = BEAMS * rows
+    half = blocks // 2
+    halves = (pl.ds(0, half), pl.ds(half, half))
+    opposite, straight = [], []
+    for d in range(2):
+        opposite.append(send_to(looked.at[across, halves[d]], opposite_half[d], col_ways[d]))
+    for d in range(2):
+        straight.append(
+            send_to(
+                looked.at[cols[d], halves[1 - d]], from_cols[d].at[halves[1 - d]], col_ways[d]
+            )
+        )
     step2 = [[send(scales1.at[d], two_s[d], d)] for d in range(2)]
     for u in range(count):
         for d in range(2):
             step2[d].append(send(items1.at[d * count + u], two[d].at[u], d))
+    for d in range(2):
+        opposite[d].wait()
+        part = part_sum[d]
+        add(part, opposite_half[d], looked.at[cols[d], halves[d]])
+        straight.append(send_to(part, from_cols[d].at[halves[d]], col_ways[d]))
+    for c in straight:
+        c.wait_recv()
+    add(col_sum, looked.at[col], from_cols[0], from_cols[1])
+    row_sends = [
+        send_to(col_sum.at[pl.ds(r * BEAMS, BEAMS)], from_rows[k], p)
+        for k, (r, p) in enumerate(zip(row_ids, row_peers))
+    ]
     step3 = []
+    chosen = []
     for d in range(2):
         for c in step2[d]:
             c.wait_recv()
@@ -178,26 +228,61 @@
         nearer = wanted_by(sign)
         farther = wanted_by(2 * sign)
         end = lowest if d == 0 else highest
-        chosen = (
+        chosen.append((
             lowest(nearer, origin, count), highest(nearer, origin, count), end(farther, origin, count)
-        )
-        for s, u in enumerate(chosen):
-            picked_s[d][s] = two_s[d][u]
-            picked[d][s] = two[d][u]
+        ))
+        for s in range(3):
+            picked_s[d][s] = two_s[d][chosen[d][s]]
+        for s in range(3):
+            picked[d][s] = two[d][chosen[d][s]]
         step3.append([send(picked_s[d], three_s[d], d)])
-        for s in (2, 0, 1):
-            step3[d].append(send(picked[d].at[s], three[d].at[s], d))
+        step3[d].append(send(picked[d].at[2], three[d].at[2], d))
+    for c in row_sends:
+        c.wait_recv()
+    add(row_sum, col_sum.at[pl.ds(row * BEAMS, BEAMS)], *from_rows)
+    reach = (BEAMS // 2, BEAMS // 2 - 1)
+
+    def block(d, distance):
+        return (BEAMS - distance) % BEAMS if d == 0 else distance
+
+    passed = [[] for _ in range(2)]
+
+    def pass_on(d):
+        k = len(passed[d])
+        if k == reach[d]:
+            return
+        at_block = block(d, reach[d] - k)
+        if k == 0:
+            src = row_sum.at[at_block]
+        else:
+            passed[d][k - 1].wait_recv()
+            hops[d][k] = row_sum[at_block] + from_beam[d][k - 1]
+            src = hops[d].at[k]
+        passed[d].append(send(src, from_beam[d].at[k], d))
+
+    for d in range(2):
+        pass_on(d)
+        step3[d].append(send(picked[d].at[0], three[d].at[0], d))
+    for d in range(2):
+        pass_on(d)
+        step3[d].append(send(picked[d].at[1], three[d].at[1], d))
     step4 = []
     for d in range(2):
         step3[d][0].wait_recv()
         step4.append(send(three_s[d].at[2], four_s[d].at[0], d))
         step3[d][1].wait_recv()
         step4.append(send(three[d].at[2], four[d].at[0], d))
+        pass_on(d)
+    for d in range(2):
+        pass_on(d)
     for d in range(2):
         for c in step3[d][2:]:
             c.wait_recv()
     for c in step4:
         c.wait_recv()
+    for d in range(2):
+        passed[d][-1].wait_recv()
+    arrived[...] = row_sum[0] + from_beam[0][reach[0] - 1] + from_beam[1][reach[1] - 1]
     mine = wanted_by(0)
     for u in range(count):
         offset = (my_beam + BEAMS - mine(u)) % BEAMS
@@ -228,30 +313,38 @@
                 )
             parents[u, h] = x
     for c in copies:
-        c.wait_send()
-
-
-def relay(wants, states, items1, scales1):
+        if id(c) not in set(map(id, opposite)):
+            c.wait_send()
+
+
+def relay(wants, states, items1, scales1, looked):
     count, heads, size, _ = states.shape
-    sends = 2 * (1 + count) + 2 * 4 + 4
+    blocks, height, width = looked.shape[1:]
+    rows = blocks // BEAMS
+    sends = 2 * (1 + count) + 2 * 4 + 4 + 6 + (rows - 1) + BEAMS - 1
     whole = pl.BlockSpec(memory_space=pltpu.VMEM)
     kept = [count, count, 3, 3, 1, 1, 3, 3]
+    parts = [blocks // 2] * 2 + [blocks] * 2 + [BEAMS] * (rows - 1) + [blocks // 2] * 2
+    parts += [BEAMS // 2] * 4 + [blocks, BEAMS]
     return pl.pallas_call(
         functools.partial(relay_kernel, count),
-        out_shape=jax.ShapeDtypeStruct(states.shape, jnp.float32),
-        in_specs=[pl.BlockSpec(memory_space=pltpu.SMEM), whole, whole, whole],
-        out_specs=whole,
+        out_shape=(
+            jax.ShapeDtypeStruct(states.shape, jnp.float32),
+            jax.ShapeDtypeStruct((height, width), looked.dtype),
+        ),
+        in_specs=[pl.BlockSpec(memory_space=pltpu.SMEM), whole, whole, whole, whole],
+        out_specs=(whole, whole),
         scratch_shapes=[
             *(pltpu.VMEM((k, heads, size, size), jnp.int16) for k in kept),
             *(pltpu.VMEM((k, heads, size), jnp.float32) for k in kept),
+            *(pltpu.VMEM((k, height, width), looked.dtype) for k in parts),
             pltpu.SemaphoreType.DMA((sends,)),
             pltpu.SemaphoreType.DMA((sends,)),
         ],
-        cost_estimate=pl.CostEstimate(flops=10**9, bytes_accessed=6 << 20, transcendentals=0),
         compiler_params=pltpu.CompilerParams(
-            collective_id=1, has_side_effects=True, vmem_limit_bytes=24 << 20
-        ),
-    )(wants, states, items1, scales1)
+            collective_id=1, has_side_effects=True, vmem_limit_bytes=40 << 20
+        ),
+    )(wants, states, items1, scales1, looked)
 
 
 def advance_kernel(parents, entries, gates, gain, readout, new_states):
@@ -321,8 +414,7 @@
     items1, scales1, table = gather(states, ids)
     every = table[:, 0, :].reshape(BEAMS, spacing, 2 * count)
     wants = lax.dynamic_slice_in_dim(every, within, 1, axis=1)[:, 0, count:]
-    order = (my_beam + BEAMS - jnp.arange(BEAMS)) % BEAMS
-    tokens = jnp.take(every[:, :, :count], order, axis=0).reshape(-1)
+    tokens = every[:, :, :count].reshape(BEAMS, spacing // ROW, ROW, count).transpose(2, 1, 0, 3).reshape(-1)
 
     vocab_rows = proj_table.shape[0]
     wide = 5 * size
@@ -342,8 +434,8 @@
         (wanted[:, None] == row_at[None, :]) & (own_head[:, None] == head_at[None, :])
     ).astype(jnp.bfloat16)
     looked = jnp.dot(onehot, padded, preferred_element_type=jnp.float32).astype(jnp.bfloat16)
-    arrived = lax.psum_scatter(looked, "beam", scatter_dimension=0, tiled=True)
-    parents = relay(wants, states, items1, scales1)
+    looked = looked.reshape(ROW, devices // ROW, count * heads, wide + size)
+    parents, arrived = relay(wants, states, items1, scales1, looked)
     arrived = arrived.astype(jnp.float32).reshape(count, heads, wide + size)
     entries = arrived[:, :, :wide].reshape(count, heads * 5, size)
     gates = arrived[:, :, wide : wide + 3].transpose(0, 2, 1).reshape(count, 3 * heads)

time: 2650 us -> 245 us (0.09)
  waiting for transfers between devices: 2420 us -> 0 us
  Pallas kernels: 200 us -> 235 us
    reduce_scatter x1 -> x0, waiting for transfers between devices: 2420 us -> none  [local(): arrived = lax.psum_scatter(looked, 'beam', scatter_dimension=0, tiled=True)]
    pallas_call x1, Pallas kernels: 93.4 us -> 129 us  [relay(): pl.pallas_call(functools.partial(relay_kernel, count), out_shape=(jax.Sha...]
  transfers between devices with their start and end apart: 1 -> 0, of which waited for: 1 -> 0; matrix products, arithmetic and copies ran while one was open for 0% -> 0% of each run, Pallas kernels for 4% -> 0%
where the time goes in v2:
time: 245 us
  Pallas kernels  235 us (96%)
  local copies, waits for them, and re-layouts  5.23 us (2%)
  matrix products  2.74 us (1%)
    pallas_call x1, Pallas kernels, relay(): pl.pallas_call(functools.partial(relay_kernel, count), out_shape=(jax.Sha...  129 us
    pallas_call x1, Pallas kernels, gather(): pl.pallas_call(functools.partial(gather_kernel, count), out_shape=(jax.Sh...  102 us

profile of v2, /device:TPU:40, one launch (start us, length us, event | category | flops | bytes accessed | tf_op | source)
XLA Modules:
  0.0 244.8 jit_solution(10897870815454219806)
XLA Ops:
  0.6 0.0 copy-start
  0.7 0.9 add_dynamic-update-slice_fusion
  1.6 0.1 pad.2.clone
  1.7 0.9 copy.15
  2.6 1.2 copy.22
  3.7 0.2 maximum_maximum_fusion
  3.9 0.0 copy-done
  3.9 102.1 %shard_map.77 = (s16[8,4,128,128]{3,2,1,0:T(8,128)(2,1)S(1)}, f32[2,4,4,128]{3,2,1,0:T(4,128)S(1)}, s32[8,8,128]{2,1,0:T(8,128)S(1)}) custom-call(f32[4,4,128,128]{3,2,1,0:T(8,128)S(1)} %copy-done, s32[8,128]{1,0:T(8,128)S(1)} %broadcast_in_dim.26.ids), custom_call_target="tpu_custom_call" | custom-call | tf_op jit(solution)/shard_map/pallas_call | solution.py:98
  106.0 0.1 reshape_squeeze.3
  106.1 0.1 constant_dynamic-slice_fusion
  106.2 0.1 sub.25
  106.3 0.1 broadcast_in_dim.27
  106.5 0.2 eq.34
  106.6 2.7 %fusion.4 = bf16[2048,768]{1,0:T(8,128)(2,1)S(1)} fusion(bf16[512,768]{1,0:T(8,128)(2,1)S(1)} %bitcast.18, s32[512]{0:T(512)S(1)} %get-tuple-element.12, s32[512]{0:T(512)S(1)} %get-tuple-element.13, s32[2048]{0:T(1024)S(1)} %add_select_fusion, s32[2048]{0:T(1024)S(1)} %eq.34), kind=kOutput, calls=%fused_computation.4 | convolution fusion | flops 1615331328 | bytes 3952640 | tf_op jit(solution)/shard_map/dot_general | solution.py:436
  109.4 128.8 %shard_map.78 = (f32[4,4,128,128]{3,2,1,0:T(8,128)S(1)}, bf16[16,768]{1,0:T(8,128)(2,1)S(1)}) custom-call(s32[8,4]{1,0:T(8,128)S(1)} %bitcast.16, f32[4,4,128,128]{3,2,1,0:T(8,128)S(1)} %copy-done, s16[8,4,128,128]{3,2,1,0:T(8,128)(2,1)S(1)} %get-tuple-element.8.items1, f32[2,4,4,128]{3,2,1,0:T(4,128)S(1)} %get-tuple-element.9.scales1, ...), custom_call_target="tpu_custom_call" | custom-call | tf_op jit(solution)/shard_map/pallas_call | solution.py:329
  238.1 0.0 copy-start.1
  238.2 1.0 copy-done.1
  239.2 0.1 copy.19
  239.3 0.1 broadcast_in_dim.29
  239.4 0.6 reshape.67.entries
  240.0 0.7 broadcast_in_dim.30.gates
  240.7 4.1 %shard_map.79 = (bf16[4,4,128]{2,1,0:T(4,128)(2,1)}, f32[4,4,128,128]{3,2,1,0:T(8,128)}) custom-call(f32[4,4,128,128]{3,2,1,0:T(8,128)} %copy-done.1, f32[4,20,128]{2,1,0:T(8,128)} %reshape.67.entries, f32[4,12,128]{2,1,0:T(8,128)} %broadcast_in_dim.30.gates, f32[4,128]{1,0:T(4,128)} %gain.1), custom_call_target="tpu_custom_call" | custom-call | tf_op jit(solution)/shard_map/pallas_call | solution.py:384
  (11 shorter events, 0.1 us)
Async XLA Ops:
  0.6 3.3 %copy-start = (f32[4,4,128,128]{3,2,1,0:T(8,128)S(1)}, f32[4,4,128,128]{3,2,1,0:T(8,128)}, u32[]{:S(2)}) copy-start(f32[4,4,128,128]{3,2,1,0:T(8,128)} %states.3) | copy-start | bytes 3145732
  238.1 1.0 copy-start.1

commit v3 on v2

v3 whole, which is shorter than its diff:
```python
import functools

import jax
import jax.numpy as jnp
from jax import lax
from jax.experimental import pallas as pl
from jax.experimental.pallas import tpu as pltpu
from jax.sharding import PartitionSpec as P

BEAMS = 8
ROW = 4
IDS = 8
LEVELS = 32767.0
EARLY = 2


def to(index):
    return dict(device_id={"beam": index}, device_id_type=pl.DeviceIdType.MESH)


def gather_kernel(count, states, ids, items, scales, table, late, q, qs, near, side, tile, sems, rsem):
    n = lax.axis_size("beam")
    me = lax.axis_index("beam")
    spacing = n // BEAMS
    rows = spacing // ROW
    my_beam, within = me // spacing, me % spacing
    row, col = within // ROW, within % ROW
    base = my_beam * spacing
    beam_peers = [(me + k * spacing) % n for k in range(1, BEAMS)]
    row_peers = [base + ((row + k) % rows) * ROW + col for k in range(1, rows)]
    col_peers = [base + row * ROW + (col + k) % ROW for k in range(1, ROW)]
    peers = beam_peers + row_peers + col_peers
    barrier = pltpu.get_barrier_semaphore()
    for p in peers:
        pl.semaphore_signal(barrier, inc=1, **to(p))
    pl.semaphore_wait(barrier, len(peers))

    copies = []
    at = [0]

    def send(src, dst, target):
        c = pltpu.make_async_remote_copy(
            src_ref=src, dst_ref=dst, send_sem=sems.at[at[0]], recv_sem=rsem.at[at[0]], **to(target)
        )
        at[0] += 1
        c.start()
        copies.append(c)
        return c

    def code(u):
        for h in range(states.shape[1]):
            x = states[u, h]
            top = jnp.maximum(jnp.max(jnp.abs(x), axis=0, keepdims=True), 1e-30)
            qs[u, h : h + 1, :] = top * (1.0 / LEVELS)
            code_to = q.at[u] if u < EARLY else late.at[u - EARLY]
            code_to[h] = lax.round(
                x * (LEVELS / top), lax.RoundingMethod.TO_NEAREST_EVEN
            ).astype(jnp.int32).astype(jnp.int16)

    first = [send(ids, near.at[k], p) for k, p in enumerate(row_peers)]
    code(0)
    ways = (beam_peers[0], beam_peers[-1])
    for d in range(2):
        send(q.at[0], items.at[d * EARLY], ways[d])
    for c in first:
        c.wait_recv()
    total = ids[...]
    for k in range(len(row_peers)):
        total = total + near[k]
    tile[0] = total
    for u in range(1, count):
        code(u)
    second = [send(tile.at[0], side.at[k], p) for k, p in enumerate(col_peers)]
    for c in second:
        c.wait_recv()
    for k in range(len(col_peers)):
        total = total + side[k]
    tile[1] = total
    for d in range(2):
        send(qs, scales.at[d], ways[d])
    for k, p in enumerate(beam_peers):
        send(tile.at[1], table.at[k + 1], p)
    for u in range(1, EARLY):
        for d in range(2):
            send(q.at[u], items.at[d * EARLY + u], ways[d])
    table[0] = total
    waited = set(map(id, first + second))
    for c in copies:
        c.wait_send()
        if id(c) not in waited:
            c.wait_recv()


def gather(states, ids):
    count, heads, size, _ = states.shape
    n = lax.axis_size("beam")
    rows = n // BEAMS // ROW
    sends = (rows - 1) + (ROW - 1) + (BEAMS - 1) + 2 * EARLY + 2
    whole = pl.BlockSpec(memory_space=pltpu.VMEM)
    return pl.pallas_call(
        functools.partial(gather_kernel, count),
        out_shape=(
            jax.ShapeDtypeStruct((2 * EARLY, heads, size, size), jnp.int16),
            jax.ShapeDtypeStruct((2, count, heads, size), jnp.float32),
            jax.ShapeDtypeStruct((BEAMS, 8, 128), jnp.int32),
            jax.ShapeDtypeStruct((count - EARLY, heads, size, size), jnp.int16),
        ),
        in_specs=[whole, whole],
        out_specs=(whole, whole, whole, whole),
        scratch_shapes=[
            pltpu.VMEM((EARLY, heads, size, size), jnp.int16),
            pltpu.VMEM((count, heads, size), jnp.float32),
            pltpu.VMEM((rows - 1, 8, 128), jnp.int32),
            pltpu.VMEM((ROW - 1, 8, 128), jnp.int32),
            pltpu.VMEM((2, 8, 128), jnp.int32),
            pltpu.SemaphoreType.DMA((sends,)),
            pltpu.SemaphoreType.DMA((sends,)),
        ],
        compiler_params=pltpu.CompilerParams(
            collective_id=0, has_side_effects=True, vmem_limit_bytes=24 << 20
        ),
    )(states, ids)


def lowest(row_of, beam, count):
    u = count - 1
    for k in range(count - 2, -1, -1):
        u = jnp.where(row_of(k) == beam, k, u)
    return u


def highest(row_of, beam, count):
    u = 0
    for k in range(1, count):
        u = jnp.where(row_of(k) == beam, k, u)
    return u


def advance(state, entry, gain):
    size = state.shape[0]
    eye = (
        lax.broadcasted_iota(jnp.int32, (size, size), 0)
        == lax.broadcasted_iota(jnp.int32, (size, size), 1)
    ).astype(jnp.float32)

    def vector(k):
        return entry(slice(k * size, (k + 1) * size))

    def unit(x):
        return x * lax.rsqrt(jnp.sum(x * x, axis=-1, keepdims=True) + 1e-06)

    def gate(k):
        x = entry(slice(5 * size + k, 5 * size + k + 1))
        return 1.0 / (1.0 + jnp.exp(-jnp.broadcast_to(x, (1, size))))

    state = gate(0) * state
    for j in range(2):
        key = unit(vector(1 + j))
        gap = jnp.sum(state * key - eye * vector(3 + j), axis=-1, keepdims=True)
        state = state - gap * (2.0 * gate(1 + j) * key)
    out = jnp.sum(state * unit(vector(0)), axis=-1, keepdims=True)
    row = jnp.sum(eye * out, axis=0, keepdims=True)
    scale = lax.rsqrt(jnp.sum(row * row, axis=-1, keepdims=True) * (1.0 / size) + 1e-05)
    return state, gain * row * scale


def relay_kernel(
    count, wants, states, items1, scales1, late, looked, gain, readout, new_states, *scratch
):
    two, three, four, picked = scratch[0:2], scratch[2:4], scratch[4:6], scratch[6:8]
    two_s, three_s, four_s, picked_s = scratch[8:10], scratch[10:12], scratch[12:14], scratch[14:16]
    one = scratch[16:18]
    opposite_half, from_cols, from_rows = scratch[18:20], scratch[20:22], scratch[22:-11]
    part_sum, hops, from_beam = scratch[-11:-9], scratch[-9:-7], scratch[-7:-5]
    col_sum, row_sum, entries, sems, rsem = scratch[-5:]
    n = lax.axis_size("beam")
    me = lax.axis_index("beam")
    spacing = n // BEAMS
    my_beam = me // spacing
    rows = spacing // ROW
    within = me % spacing
    row, col = within // ROW, within % ROW
    base = my_beam * spacing
    ways = ((me + spacing) % n, (me + n - spacing) % n)
    cols = ((col + 1) % ROW, (col + ROW - 1) % ROW)
    across = (col + 2) % ROW
    col_ways = [base + row * ROW + c for c in cols]
    row_ids = [(row + k) % rows for k in range(1, rows)]
    row_peers = [base + r * ROW + col for r in row_ids]
    barrier = pltpu.get_barrier_semaphore()
    peers = [*ways, *col_ways, *row_peers]
    for p in peers:
        pl.semaphore_signal(barrier, inc=1, **to(p))
    pl.semaphore_wait(barrier, len(peers))

    def beam(d):
        return (my_beam + BEAMS + d) % BEAMS

    def wanted_by(d):
        return lambda u: wants[(BEAMS - d) % BEAMS, u]

    copies = []
    at = [0]

    def send_to(src, dst, target):
        c = pltpu.make_async_remote_copy(
            src_ref=src, dst_ref=dst, send_sem=sems.at[at[0]], recv_sem=rsem.at[at[0]], **to(target)
        )
        at[0] += 1
        c.start()
        copies.append(c)
        return c

    def send(src, dst, way):
        return send_to(src, dst, ways[way])

    def add(dst, *srcs):
        def step(i, _):
            x = srcs[0][i]
            for y in srcs[1:]:
                x = x + y[i]
            dst[i] = x
            return 0

        lax.fori_loop(0, dst.shape[0], step, 0)

    blocks = BEAMS * rows
    half = blocks // 2
    halves = (pl.ds(0, half), pl.ds(half, half))
    opposite, straight = [], []
    for d in range(2):
        opposite.append(send_to(looked.at[across, halves[d]], opposite_half[d], col_ways[d]))
    for d in range(2):
        straight.append(
            send_to(
                looked.at[cols[d], halves[1 - d]], from_cols[d].at[halves[1 - d]], col_ways[d]
            )
        )
    step1 = [[] for _ in range(2)]
    for u in range(EARLY, count):
        for d in range(2):
            step1[d].append(send(late.at[u - EARLY], one[d].at[u - EARLY], d))
    step2 = [[send(scales1.at[d], two_s[d], d)] for d in range(2)]

    def forward(u):
        for d in range(2):
            if u < EARLY:
                src = items1.at[d * EARLY + u]
            else:
                step1[d][u - EARLY].wait_recv()
                src = one[d].at[u - EARLY]
            step2[d].append(send(src, two[d].at[u], d))

    forward(0)
    for d in range(2):
        opposite[d].wait()
        part = part_sum[d]
        add(part, opposite_half[d], looked.at[cols[d], halves[d]])
        straight.append(send_to(part, from_cols[d].at[halves[d]], col_ways[d]))
    for c in straight:
        c.wait_recv()
    add(col_sum, looked.at[col], from_cols[0], from_cols[1])
    row_sends = [
        send_to(col_sum.at[pl.ds(r * BEAMS, BEAMS)], from_rows[k], p)
        for k, (r, p) in enumerate(zip(row_ids, row_peers))
    ]
    for u in range(1, EARLY):
        forward(u)
    for c in row_sends:
        c.wait_recv()
    add(row_sum, col_sum.at[pl.ds(row * BEAMS, BEAMS)], *from_rows)
    reach = (BEAMS // 2, BEAMS // 2 - 1)
    passed = [[] for _ in range(2)]

    def pass_on():
        for d in range(2):
            k = len(passed[d])
            if k == reach[d]:
                continue
            distance = reach[d] - k
            block = BEAMS - distance if d == 0 else distance
            if k == 0:
                src = row_sum.at[block]
            else:
                passed[d][k - 1].wait_recv()
                hops[d][k] = row_sum[block] + from_beam[d][k - 1]
                src = hops[d].at[k]
            passed[d].append(send(src, from_beam[d].at[k], d))

    pass_on()
    for u in range(EARLY, count):
        forward(u)
        pass_on()
    step3 = []
    for d in range(2):
        for c in step2[d]:
            c.wait_recv()
        sign = 1 if d == 0 else -1
        origin = beam(-2 * sign)
        nearer = wanted_by(sign)
        farther = wanted_by(2 * sign)
        end = lowest if d == 0 else highest
        chosen = (
            lowest(nearer, origin, count), highest(nearer, origin, count), end(farther, origin, count)
        )
        for s in range(3):
            picked_s[d][s] = two_s[d][chosen[s]]
        for s in range(3):
            picked[d][s] = two[d][chosen[s]]
        step3.append([send(picked_s[d], three_s[d], d)])
        step3[d].append(send(picked[d].at[2], three[d].at[2], d))
    while any(len(passed[d]) < reach[d] for d in range(2)):
        pass_on()
    for d in range(2):
        step3[d].append(send(picked[d].at[0], three[d].at[0], d))
    step4 = []
    for d in range(2):
        step3[d][0].wait_recv()
        step4.append(send(three_s[d].at[2], four_s[d].at[0], d))
        step3[d][1].wait_recv()
        step4.append(send(three[d].at[2], four[d].at[0], d))
    for d in range(2):
        step3[d].append(send(picked[d].at[1], three[d].at[1], d))
    for d in range(2):
        passed[d][-1].wait_recv()
    entries[...] = (
        row_sum[0] + from_beam[0][reach[0] - 1] + from_beam[1][reach[1] - 1]
    ).astype(jnp.float32)
    for c in step4:
        c.wait_recv()
    for d in range(2):
        for c in step3[d][2:]:
            c.wait_recv()
    mine = wanted_by(0)
    for u in range(count):
        offset = (my_beam + BEAMS - mine(u)) % BEAMS
        third = [jnp.where(lowest(mine, beam(d), count) == u, 0, 1) for d in (-3, 3)]
        middle = lowest(mine, beam(4), count) == u
        rows_out = []
        for h in range(states.shape[1]):
            x = states[u, h]
            line = u * states.shape[1] + h

            def take(x, when, code, scale):
                return jnp.where(when, code.astype(jnp.int32).astype(jnp.float32) * scale, x)

            for d in range(2):
                near = items1[d * EARLY + u, h] if u < EARLY else one[d][u - EARLY, h]
                x = take(x, offset == (1, BEAMS - 1)[d], near, scales1[d, u, h : h + 1, :])
                x = take(
                    x, offset == (2, BEAMS - 2)[d], two[d][u, h], two_s[d][u, h : h + 1, :]
                )
                x = take(
                    x, offset == (3, BEAMS - 3)[d],
                    three[d][third[d], h], three_s[d][third[d], h : h + 1, :],
                )
                x = take(
                    x, (offset == 4) & (middle if d == 0 else jnp.logical_not(middle)),
                    four[d][0, h], four_s[d][0, h : h + 1, :],
                )
            state, out = advance(x, lambda k: entries[line : line + 1, k], gain[h : h + 1, :])
            new_states[u, h] = state
            rows_out.append(out)
        readout[u] = jnp.concatenate(rows_out, axis=0).astype(jnp.bfloat16)
    for c in copies:
        if id(c) not in set(map(id, opposite)):
            c.wait_send()


def relay(wants, states, items1, scales1, late, looked, gain):
    count, heads, size, _ = states.shape
    blocks, height, width = looked.shape[1:]
    rows = blocks // BEAMS
    sends = 2 * (1 + count) + 2 * (count - EARLY) + 2 * 4 + 4 + 6 + (rows - 1) + BEAMS - 1
    whole = pl.BlockSpec(memory_space=pltpu.VMEM)
    kept = [count, count, 3, 3, 1, 1, 3, 3]
    parts = [blocks // 2] * 2 + [blocks] * 2 + [BEAMS] * (rows - 1) + [blocks // 2] * 2
    parts += [BEAMS // 2] * 4 + [blocks, BEAMS]
    return pl.pallas_call(
        functools.partial(relay_kernel, count),
        out_shape=(
            jax.ShapeDtypeStruct((count, heads, size), jnp.bfloat16),
            jax.ShapeDtypeStruct(states.shape, jnp.float32),
        ),
        in_specs=[pl.BlockSpec(memory_space=pltpu.SMEM)] + [whole] * 6,
        out_specs=(whole, whole),
        scratch_shapes=[
            *(pltpu.VMEM((k, heads, size, size), jnp.int16) for k in kept),
            *(pltpu.VMEM((k, heads, size), jnp.float32) for k in kept),
            *(pltpu.VMEM((count - EARLY, heads, size, size), jnp.int16) for _ in range(2)),
            *(pltpu.VMEM((k, height, width), looked.dtype) for k in parts),
            pltpu.VMEM((height, width), jnp.float32),
            pltpu.SemaphoreType.DMA((sends,)),
            pltpu.SemaphoreType.DMA((sends,)),
        ],
        compiler_params=pltpu.CompilerParams(
            collective_id=1, has_side_effects=True, vmem_limit_bytes=40 << 20
        ),
    )(wants, states, items1, scales1, late, looked, gain)


def local(states, parent_beam, next_token, proj_table, gate_table, gain):
    count, heads, size, _ = states.shape
    devices = lax.axis_size("beam")
    spacing = devices // BEAMS
    position = lax.axis_index("beam")
    my_beam, within = position // spacing, position % spacing
    lanes = jnp.zeros((128,), jnp.int32)
    mine = jnp.concatenate([next_token, parent_beam])
    lanes = lax.dynamic_update_slice(lanes, mine, (within * 2 * count,))
    ids = jnp.broadcast_to(lanes[None, :], (8, 128))
    items1, scales1, table, late = gather(states, ids)
    every = table[:, 0, :].reshape(BEAMS, spacing, 2 * count)
    wants = lax.dynamic_slice_in_dim(every, within, 1, axis=1)[:, 0, count:]
    tokens = every[:, :, :count].reshape(BEAMS, spacing // ROW, ROW, count).transpose(2, 1, 0, 3).reshape(-1)

    vocab_rows = proj_table.shape[0]
    wide = 5 * size
    padded = jnp.concatenate(
        [
            proj_table.transpose(1, 0, 2),
            gate_table.transpose(2, 0, 1),
            jnp.zeros((heads, vocab_rows, size - 3), proj_table.dtype),
        ],
        axis=2,
    ).reshape(heads * vocab_rows, wide + size)
    wanted = jnp.repeat(tokens - position * vocab_rows, heads)
    head_at = jnp.arange(heads * vocab_rows, dtype=jnp.int32) // vocab_rows
    row_at = jnp.arange(heads * vocab_rows, dtype=jnp.int32) % vocab_rows
    own_head = jnp.arange(wanted.shape[0], dtype=jnp.int32) % heads
    onehot = (
        (wanted[:, None] == row_at[None, :]) & (own_head[:, None] == head_at[None, :])
    ).astype(jnp.bfloat16)
    looked = jnp.dot(onehot, padded, preferred_element_type=jnp.float32).astype(jnp.bfloat16)
    looked = looked.reshape(ROW, devices // ROW, count * heads, wide + size)
    return relay(wants, states, items1, scales1, late, looked, gain)


def solution(mesh):
    return jax.shard_map(
        local,
        mesh=mesh,
        in_specs=(
            P(("groups", "beam"), "mp", None, None),
            P(("groups", "beam")),
            P(("groups", "beam")),
            P("beam", "mp", None),
            P("beam", None, "mp"),
            P("mp", None),
        ),
        out_specs=(P(("groups", "beam"), "mp", None), P(("groups", "beam"), "mp", None, None)),
        check_vma=False,
    )
```

time: 245 us -> 248 us (1.012)
  the two profiles are of different devices: /device:TPU:40 before, /device:TPU:37 now
where the time goes in v3:
time: 248 us
  Pallas kernels  239 us (96%)
  local copies, waits for them, and re-layouts  4.29 us (2%)
  matrix products  2.74 us (1%)
    pallas_call x1, Pallas kernels, relay(): pl.pallas_call(functools.partial(relay_kernel, count), out_shape=(jax.Sha...  164 us
    pallas_call x1, Pallas kernels, gather(): pl.pallas_call(functools.partial(gather_kernel, count), out_shape=(jax.Sh...  75.2 us

profile of v3, /device:TPU:37, one launch (start us, length us, event | category | flops | bytes accessed | tf_op | source)
XLA Modules:
  0.0 248.0 jit_solution(2457215210055687837)
XLA Ops:
  0.6 0.0 copy-start
  0.7 0.9 add_dynamic-update-slice_fusion
  1.6 0.1 pad.2.clone
  1.7 0.9 copy.14
  2.5 1.2 copy.19
  3.7 0.1 maximum_maximum_fusion
  3.9 0.0 copy-done
  3.9 75.2 %shard_map.77 = (s16[4,4,128,128]{3,2,1,0:T(8,128)(2,1)S(1)}, f32[2,4,4,128]{3,2,1,0:T(4,128)S(1)}, s32[8,8,128]{2,1,0:T(8,128)S(1)}, s16[2,4,128,128]{3,2,1,0:T(8,128)(2,1)S(1)}) custom-call(f32[4,4,128,128]{3,2,1,0:T(8,128)S(1)} %copy-done, s32[8,128]{1,0:T(8,128)S(1)} %broadcast_in_dim.9.ids), custom_call_target="tpu_custom_call" | custom-call | tf_op jit(solution)/shard_map/pallas_call | solution.py:100
  79.1 0.1 reshape_squeeze.3
  79.2 0.1 constant_dynamic-slice_fusion
  79.3 0.1 sub.25
  79.4 0.1 broadcast_in_dim.20
  79.6 0.2 eq.34
  79.7 0.0 copy-start.1
  79.7 2.7 %fusion.4 = bf16[2048,768]{1,0:T(8,128)(2,1)S(1)} fusion(bf16[512,768]{1,0:T(8,128)(2,1)S(1)} %bitcast.17, s32[512]{0:T(512)S(1)} %get-tuple-element.10, s32[512]{0:T(512)S(1)} %get-tuple-element.11, s32[2048]{0:T(1024)S(1)} %add_select_fusion, s32[2048]{0:T(1024)S(1)} %eq.34), kind=kOutput, calls=%fused_computation.4 | convolution fusion | flops 1615331328 | bytes 3952640 | tf_op jit(solution)/shard_map/dot_general | solution.py:434
  82.5 0.0 copy-done.1
  82.5 163.9 %shard_map.78 = (bf16[4,4,128]{2,1,0:T(4,128)(2,1)S(1)}, f32[4,4,128,128]{3,2,1,0:T(8,128)S(1)}) custom-call(s32[8,4]{1,0:T(8,128)S(1)} %bitcast.15, f32[4,4,128,128]{3,2,1,0:T(8,128)S(1)} %copy-done, s16[4,4,128,128]{3,2,1,0:T(8,128)(2,1)S(1)} %get-tuple-element.7.items1, f32[2,4,4,128]{3,2,1,0:T(4,128)S(1)} %get-tuple-element.8.scales1, ...), custom_call_target="tpu_custom_call" | custom-call | tf_op jit(solution)/shard_map/pallas_call | solution.py:379
  246.4 0.6 copy.24
  247.0 1.0 copy.25
  (8 shorter events, 0.1 us)
Async XLA Ops:
  0.6 3.2 %copy-start = (f32[4,4,128,128]{3,2,1,0:T(8,128)S(1)}, f32[4,4,128,128]{3,2,1,0:T(8,128)}, u32[]{:S(2)}) copy-start(f32[4,4,128,128]{3,2,1,0:T(8,128)} %states.3) | copy-start | bytes 3145732
  79.7 2.8 %copy-start.1 = (f32[4,128]{1,0:T(4,128)S(1)}, f32[4,128]{1,0:T(4,128)}, u32[]{:S(2)}) copy-start(f32[4,128]{1,0:T(4,128)} %gain.1) | copy-start | bytes 6148

commit v4 on v3

--- a/solution.py
+++ b/solution.py
@@ -170,9 +170,9 @@
     two, three, four, picked = scratch[0:2], scratch[2:4], scratch[4:6], scratch[6:8]
     two_s, three_s, four_s, picked_s = scratch[8:10], scratch[10:12], scratch[12:14], scratch[14:16]
     one = scratch[16:18]
-    opposite_half, from_cols, from_rows = scratch[18:20], scratch[20:22], scratch[22:-11]
-    part_sum, hops, from_beam = scratch[-11:-9], scratch[-9:-7], scratch[-7:-5]
-    col_sum, row_sum, entries, sems, rsem = scratch[-5:]
+    opposite_half, from_cols, part_sum = scratch[18:20], scratch[20:22], scratch[22:24]
+    hops, from_row = scratch[24:26], scratch[26:28]
+    col_sum, entries, sems, rsem = scratch[28:]
     n = lax.axis_size("beam")
     me = lax.axis_index("beam")
     spacing = n // BEAMS
@@ -185,10 +185,9 @@
     cols = ((col + 1) % ROW, (col + ROW - 1) % ROW)
     across = (col + 2) % ROW
     col_ways = [base + row * ROW + c for c in cols]
-    row_ids = [(row + k) % rows for k in range(1, rows)]
-    row_peers = [base + r * ROW + col for r in row_ids]
+    row_ways = ((me + ROW) % n, (me + n - ROW) % n)
     barrier = pltpu.get_barrier_semaphore()
-    peers = [*ways, *col_ways, *row_peers]
+    peers = [*ways, *col_ways, *row_ways]
     for p in peers:
         pl.semaphore_signal(barrier, inc=1, **to(p))
     pl.semaphore_wait(barrier, len(peers))
@@ -236,22 +235,69 @@
                 looked.at[cols[d], halves[1 - d]], from_cols[d].at[halves[1 - d]], col_ways[d]
             )
         )
-    step1 = [[] for _ in range(2)]
-    for u in range(EARLY, count):
-        for d in range(2):
-            step1[d].append(send(late.at[u - EARLY], one[d].at[u - EARLY], d))
-    step2 = [[send(scales1.at[d], two_s[d], d)] for d in range(2)]
-
-    def forward(u):
+    heads = states.shape[1]
+    step1 = [{}, {}]
+    step2 = [{}, {}]
+    step3 = [{}, {}]
+    step4 = [{}, {}]
+
+    def send1(u, h):
+        for d in range(2):
+            step1[d][u, h] = send(late.at[u - EARLY, h], one[d].at[u - EARLY, h], d)
+
+    def send2(u, h):
         for d in range(2):
             if u < EARLY:
-                src = items1.at[d * EARLY + u]
+                src = items1.at[d * EARLY + u, h]
             else:
-                step1[d][u - EARLY].wait_recv()
-                src = one[d].at[u - EARLY]
-            step2[d].append(send(src, two[d].at[u], d))
-
-    forward(0)
+                step1[d][u, h].wait_recv()
+                src = one[d].at[u - EARLY, h]
+            step2[d][u, h] = send(src, two[d].at[u, h], d)
+
+    def pick():
+        for d in range(2):
+            for c in step2[d].values():
+                c.wait_recv()
+            sign = 1 if d == 0 else -1
+            origin = beam(-2 * sign)
+            nearer = wanted_by(sign)
+            farther = wanted_by(2 * sign)
+            end = lowest if d == 0 else highest
+            chosen = (
+                lowest(nearer, origin, count),
+                highest(nearer, origin, count),
+                end(farther, origin, count),
+            )
+            for s in (2, 0, 1):
+                picked_s[d][s] = two_s[d][chosen[s]]
+                picked[d][s] = two[d][chosen[s]]
+            step3[d]["scales"] = send(picked_s[d], three_s[d], d)
+
+    def send3(s, h):
+        for d in range(2):
+            step3[d][s, h] = send(picked[d].at[s, h], three[d].at[s, h], d)
+
+    def send4(h):
+        for d in range(2):
+            if h == 0:
+                step3[d]["scales"].wait_recv()
+                step4[d]["scales"] = send(three_s[d].at[2], four_s[d].at[0], d)
+            step3[d][2, h].wait_recv()
+            step4[d][h] = send(three[d].at[2, h], four[d].at[0, h], d)
+
+    each = range(heads)
+    todo = [functools.partial(send1, u, h) for u in range(EARLY, count) for h in each]
+    todo += [functools.partial(send2, 0, h) for h in each]
+    ahead = len(todo)
+    todo += [functools.partial(send2, u, h) for u in range(1, count) for h in each]
+    todo += [functools.partial(send3, s, h) for s in (2, 0) for h in each]
+    picking = todo[len(todo) - 2 * heads]
+    todo += [functools.partial(send4, h) for h in each]
+    todo += [functools.partial(send3, 1, h) for h in each]
+    for d in range(2):
+        step2[d]["scales"] = send(scales1.at[d], two_s[d], d)
+    for unit in todo[:ahead]:
+        unit()
     for d in range(2):
         opposite[d].wait()
         part = part_sum[d]
@@ -260,76 +306,46 @@
     for c in straight:
         c.wait_recv()
     add(col_sum, looked.at[col], from_cols[0], from_cols[1])
-    row_sends = [
-        send_to(col_sum.at[pl.ds(r * BEAMS, BEAMS)], from_rows[k], p)
-        for k, (r, p) in enumerate(zip(row_ids, row_peers))
-    ]
-    for u in range(1, EARLY):
-        forward(u)
-    for c in row_sends:
-        c.wait_recv()
-    add(row_sum, col_sum.at[pl.ds(row * BEAMS, BEAMS)], *from_rows)
-    reach = (BEAMS // 2, BEAMS // 2 - 1)
+
+    reach = (blocks // 2, blocks // 2 - 1)
     passed = [[] for _ in range(2)]
+
+    def block(distance):
+        z = (my_beam * rows + row + blocks + distance) % blocks
+        return (z % rows) * BEAMS + (my_beam + BEAMS - z // rows) % BEAMS
 
     def pass_on():
         for d in range(2):
             k = len(passed[d])
             if k == reach[d]:
                 continue
-            distance = reach[d] - k
-            block = BEAMS - distance if d == 0 else distance
+            at_block = block(reach[d] - k if d == 0 else k - reach[d])
             if k == 0:
-                src = row_sum.at[block]
+                src = col_sum.at[at_block]
             else:
                 passed[d][k - 1].wait_recv()
-                hops[d][k] = row_sum[block] + from_beam[d][k - 1]
+                hops[d][k] = col_sum[at_block] + from_row[d][k - 1]
                 src = hops[d].at[k]
-            passed[d].append(send(src, from_beam[d].at[k], d))
-
+            passed[d].append(send_to(src, from_row[d].at[k], row_ways[d]))
+
+    rest = todo[ahead:]
     pass_on()
-    for u in range(EARLY, count):
-        forward(u)
-        pass_on()
-    step3 = []
-    for d in range(2):
-        for c in step2[d]:
-            c.wait_recv()
-        sign = 1 if d == 0 else -1
-        origin = beam(-2 * sign)
-        nearer = wanted_by(sign)
-        farther = wanted_by(2 * sign)
-        end = lowest if d == 0 else highest
-        chosen = (
-            lowest(nearer, origin, count), highest(nearer, origin, count), end(farther, origin, count)
-        )
-        for s in range(3):
-            picked_s[d][s] = two_s[d][chosen[s]]
-        for s in range(3):
-            picked[d][s] = two[d][chosen[s]]
-        step3.append([send(picked_s[d], three_s[d], d)])
-        step3[d].append(send(picked[d].at[2], three[d].at[2], d))
-    while any(len(passed[d]) < reach[d] for d in range(2)):
-        pass_on()
-    for d in range(2):
-        step3[d].append(send(picked[d].at[0], three[d].at[0], d))
-    step4 = []
-    for d in range(2):
-        step3[d][0].wait_recv()
-        step4.append(send(three_s[d].at[2], four_s[d].at[0], d))
-        step3[d][1].wait_recv()
-        step4.append(send(three[d].at[2], four[d].at[0], d))
-    for d in range(2):
-        step3[d].append(send(picked[d].at[1], three[d].at[1], d))
+    for i, unit in enumerate(rest):
+        if unit is picking:
+            pick()
+        unit()
+        while len(passed[0]) < min(reach[0], 1 + (i + 1) * reach[0] // len(rest)):
+            pass_on()
     for d in range(2):
         passed[d][-1].wait_recv()
     entries[...] = (
-        row_sum[0] + from_beam[0][reach[0] - 1] + from_beam[1][reach[1] - 1]
+        col_sum[block(0)] + from_row[0][reach[0] - 1] + from_row[1][reach[1] - 1]
     ).astype(jnp.float32)
-    for c in step4:
-        c.wait_recv()
-    for d in range(2):
-        for c in step3[d][2:]:
+    for d in range(2):
+        for key, c in step3[d].items():
+            if key != "scales" and key[0] != 2:
+                c.wait_recv()
+        for c in step4[d].values():
             c.wait_recv()
     mine = wanted_by(0)
     for u in range(count):
@@ -370,12 +386,10 @@
 def relay(wants, states, items1, scales1, late, looked, gain):
     count, heads, size, _ = states.shape
     blocks, height, width = looked.shape[1:]
-    rows = blocks // BEAMS
-    sends = 2 * (1 + count) + 2 * (count - EARLY) + 2 * 4 + 4 + 6 + (rows - 1) + BEAMS - 1
+    sends = 2 * heads * (count - EARLY + count + 4) + 2 * 3 + 6 + blocks - 1
     whole = pl.BlockSpec(memory_space=pltpu.VMEM)
     kept = [count, count, 3, 3, 1, 1, 3, 3]
-    parts = [blocks // 2] * 2 + [blocks] * 2 + [BEAMS] * (rows - 1) + [blocks // 2] * 2
-    parts += [BEAMS // 2] * 4 + [blocks, BEAMS]
+    parts = [blocks // 2] * 2 + [blocks] * 2 + [blocks // 2] * 6 + [blocks]
     return pl.pallas_call(
         functools.partial(relay_kernel, count),
         out_shape=(

time: 248 us -> 244 us (0.984)
  the two profiles are of different devices: /device:TPU:37 before, /device:TPU:44 now
where the time goes in v4:
time: 244 us
  Pallas kernels  235 us (96%)
  local copies, waits for them, and re-layouts  4.29 us (2%)
  matrix products  2.74 us (1%)
    pallas_call x1, Pallas kernels, relay(): pl.pallas_call(functools.partial(relay_kernel, count), out_shape=(jax.Sha...  150 us
    pallas_call x1, Pallas kernels, gather(): pl.pallas_call(functools.partial(gather_kernel, count), out_shape=(jax.Sh...  85.4 us

profile of v4, /device:TPU:44, one launch (start us, length us, event | category | flops | bytes accessed | tf_op | source)
XLA Modules:
  0.0 244.2 jit_solution(10792713570282800590)
XLA Ops:
  0.6 0.0 copy-start
  0.7 0.9 add_dynamic-update-slice_fusion
  1.6 0.1 pad.2.clone
  1.7 0.9 copy.14
  2.5 1.2 copy.19
  3.7 0.1 maximum_maximum_fusion
  3.9 0.0 copy-done
  3.9 85.4 %shard_map.77 = (s16[4,4,128,128]{3,2,1,0:T(8,128)(2,1)S(1)}, f32[2,4,4,128]{3,2,1,0:T(4,128)S(1)}, s32[8,8,128]{2,1,0:T(8,128)S(1)}, s16[2,4,128,128]{3,2,1,0:T(8,128)(2,1)S(1)}) custom-call(f32[4,4,128,128]{3,2,1,0:T(8,128)S(1)} %copy-done, s32[8,128]{1,0:T(8,128)S(1)} %broadcast_in_dim.9.ids), custom_call_target="tpu_custom_call" | custom-call | tf_op jit(solution)/shard_map/pallas_call | solution.py:100
  89.3 0.1 reshape_squeeze.3
  89.4 0.1 constant_dynamic-slice_fusion
  89.5 0.1 sub.25
  89.6 0.1 broadcast_in_dim.20
  89.7 0.2 eq.34
  89.9 0.0 copy-start.1
  89.9 2.7 %fusion.4 = bf16[2048,768]{1,0:T(8,128)(2,1)S(1)} fusion(bf16[512,768]{1,0:T(8,128)(2,1)S(1)} %bitcast.17, s32[512]{0:T(512)S(1)} %get-tuple-element.10, s32[512]{0:T(512)S(1)} %get-tuple-element.11, s32[2048]{0:T(1024)S(1)} %add_select_fusion, s32[2048]{0:T(1024)S(1)} %eq.34), kind=kOutput, calls=%fused_computation.4 | convolution fusion | flops 1615331328 | bytes 3952640 | tf_op jit(solution)/shard_map/dot_general | solution.py:448
  92.6 0.0 copy-done.1
  92.7 150.0 %shard_map.78 = (bf16[4,4,128]{2,1,0:T(4,128)(2,1)S(1)}, f32[4,4,128,128]{3,2,1,0:T(8,128)S(1)}) custom-call(s32[8,4]{1,0:T(8,128)S(1)} %bitcast.15, f32[4,4,128,128]{3,2,1,0:T(8,128)S(1)} %copy-done, s16[4,4,128,128]{3,2,1,0:T(8,128)(2,1)S(1)} %get-tuple-element.7.items1, f32[2,4,4,128]{3,2,1,0:T(4,128)S(1)} %get-tuple-element.8.scales1, ...), custom_call_target="tpu_custom_call" | custom-call | tf_op jit(solution)/shard_map/pallas_call | solution.py:393
  242.6 0.6 copy.24
  243.2 1.0 copy.25
  (8 shorter events, 0.1 us)
Async XLA Ops:
  0.6 3.2 %copy-start = (f32[4,4,128,128]{3,2,1,0:T(8,128)S(1)}, f32[4,4,128,128]{3,2,1,0:T(8,128)}, u32[]{:S(2)}) copy-start(f32[4,4,128,128]{3,2,1,0:T(8,128)} %states.3) | copy-start | bytes 3145732
  89.9 2.8 %copy-start.1 = (f32[4,128]{1,0:T(4,128)S(1)}, f32[4,128]{1,0:T(4,128)}, u32[]{:S(2)}) copy-start(f32[4,128]{1,0:T(4,128)} %gain.1) | copy-start | bytes 6148

commit v5 on v4

v5 whole, which is shorter than its diff:
```python
import functools

import jax
import jax.numpy as jnp
from jax import lax
from jax.experimental import pallas as pl
from jax.experimental.pallas import tpu as pltpu
from jax.sharding import PartitionSpec as P

BEAMS = 8
ROW = 4
IDS = 8
LEVELS = 32767.0


def to(index):
    return dict(device_id={"beam": index}, device_id_type=pl.DeviceIdType.MESH)


def lowest(row_of, beam, count):
    u = count - 1
    for k in range(count - 2, -1, -1):
        u = jnp.where(row_of(k) == beam, k, u)
    return u


def highest(row_of, beam, count):
    u = 0
    for k in range(1, count):
        u = jnp.where(row_of(k) == beam, k, u)
    return u


def advance(state, entry, gain):
    size = state.shape[0]
    eye = (
        lax.broadcasted_iota(jnp.int32, (size, size), 0)
        == lax.broadcasted_iota(jnp.int32, (size, size), 1)
    ).astype(jnp.float32)

    def vector(k):
        return entry(slice(k * size, (k + 1) * size))

    def unit(x):
        return x * lax.rsqrt(jnp.sum(x * x, axis=-1, keepdims=True) + 1e-06)

    def gate(k):
        x = entry(slice(5 * size + k, 5 * size + k + 1))
        return 1.0 / (1.0 + jnp.exp(-jnp.broadcast_to(x, (1, size))))

    state = gate(0) * state
    for j in range(2):
        key = unit(vector(1 + j))
        gap = jnp.sum(state * key - eye * vector(3 + j), axis=-1, keepdims=True)
        state = state - gap * (2.0 * gate(1 + j) * key)
    out = jnp.sum(state * unit(vector(0)), axis=-1, keepdims=True)
    row = jnp.sum(eye * out, axis=0, keepdims=True)
    scale = lax.rsqrt(jnp.sum(row * row, axis=-1, keepdims=True) * (1.0 / size) + 1e-05)
    return state, gain * row * scale


def step_kernel(count, states, ids, rows_of_tokens, gain, readout, new_states, *scratch):
    two, three, four, picked = scratch[0:2], scratch[2:4], scratch[4:6], scratch[6:8]
    two_s, three_s, four_s, picked_s = scratch[8:10], scratch[10:12], scratch[12:14], scratch[14:16]
    one, one_s = scratch[16:18], scratch[18:20]
    opposite_half, from_cols, part_sum = scratch[20:22], scratch[22:24], scratch[24:26]
    hops, from_row = scratch[26:28], scratch[28:30]
    col_sum, entries, looked, q, qs, near, side, tile, table, wants, copied, sems, rsem = scratch[30:]
    n = lax.axis_size("beam")
    me = lax.axis_index("beam")
    spacing = n // BEAMS
    my_beam = me // spacing
    rows = spacing // ROW
    within = me % spacing
    row, col = within // ROW, within % ROW
    base = my_beam * spacing
    ways = ((me + spacing) % n, (me + n - spacing) % n)
    cols = ((col + 1) % ROW, (col + ROW - 1) % ROW)
    across = (col + 2) % ROW
    col_ways = [base + row * ROW + c for c in cols]
    row_ways = ((me + ROW) % n, (me + n - ROW) % n)
    barrier = pltpu.get_barrier_semaphore()
    beam_peers = [(me + k * spacing) % n for k in range(1, BEAMS)]
    row_peers = [base + ((row + k) % rows) * ROW + col for k in range(1, rows)]
    col_peers = [base + row * ROW + (col + k) % ROW for k in range(1, ROW)]
    peers = [*beam_peers, *row_peers, *col_peers, *row_ways]
    for p in peers:
        pl.semaphore_signal(barrier, inc=1, **to(p))
    pl.semaphore_wait(barrier, len(peers))

    def beam(d):
        return (my_beam + BEAMS + d) % BEAMS

    def wanted_by(d):
        return lambda u: wants[(BEAMS - d) % BEAMS, 2, within * count + u]

    copies = []
    at = [0]

    def send_to(src, dst, target):
        c = pltpu.make_async_remote_copy(
            src_ref=src, dst_ref=dst, send_sem=sems.at[at[0]], recv_sem=rsem.at[at[0]], **to(target)
        )
        at[0] += 1
        c.start()
        copies.append(c)
        return c

    def send(src, dst, way):
        return send_to(src, dst, ways[way])

    def add(dst, *srcs):
        def step(i, _):
            x = srcs[0][i]
            for y in srcs[1:]:
                x = x + y[i]
            dst[i] = x
            return 0

        lax.fori_loop(0, dst.shape[0], step, 0)

    blocks = BEAMS * rows
    half = blocks // 2
    halves = (pl.ds(0, half), pl.ds(half, half))

    def code(u):
        for h in range(states.shape[1]):
            x = states[u, h]
            top = jnp.maximum(jnp.max(jnp.abs(x), axis=0, keepdims=True), 1e-30)
            qs[u, h : h + 1, :] = top * (1.0 / LEVELS)
            q[u, h] = lax.round(
                x * (LEVELS / top), lax.RoundingMethod.TO_NEAREST_EVEN
            ).astype(jnp.int32).astype(jnp.int16)

    def look_up():
        lines = rows_of_tokens.shape[0]
        heads = states.shape[1]
        vocab_rows = lines // heads
        lanes = tile.shape[-1]
        per = count * heads
        head = lax.rem(lax.broadcasted_iota(jnp.int32, (1, lanes), 1), heads)
        at_line = lax.broadcasted_iota(jnp.int32, (lines, lanes), 0)
        for k in range(BEAMS):
            for r in range(spacing * per // lanes):
                token = table[k, r : r + 1, :] - me * vocab_rows
                mine = (token >= 0) & (token < vocab_rows)
                line = jnp.where(mine, token + head * vocab_rows, -1)
                onehot = jnp.where(at_line == line, 1.0, 0.0).astype(jnp.bfloat16)
                out = lax.dot_general(
                    onehot, rows_of_tokens[...], (((0,), (0,)), ((), ())),
                    preferred_element_type=jnp.float32,
                ).astype(looked.dtype)
                for w in range(lanes // per):
                    dev = r * (lanes // per) + w
                    looked[dev % ROW, (dev // ROW) * BEAMS + k] = out[w * per : (w + 1) * per, :]

    heads = states.shape[1]
    step1 = [{}, {}]
    step2 = [{}, {}]
    step3 = [{}, {}]
    step4 = [{}, {}]

    def send1(u, h):
        for d in range(2):
            step1[d][u, h] = send(q.at[u, h], one[d].at[u, h], d)

    def send2(u, h):
        for d in range(2):
            step1[d][u, h].wait_recv()
            step2[d][u, h] = send(one[d].at[u, h], two[d].at[u, h], d)

    def pick():
        for d in range(2):
            for c in step2[d].values():
                c.wait_recv()
            sign = 1 if d == 0 else -1
            origin = beam(-2 * sign)
            nearer = wanted_by(sign)
            farther = wanted_by(2 * sign)
            end = lowest if d == 0 else highest
            chosen = (
                lowest(nearer, origin, count),
                highest(nearer, origin, count),
                end(farther, origin, count),
            )
            for s in (2, 0, 1):
                picked_s[d][s] = two_s[d][chosen[s]]
                picked[d][s] = two[d][chosen[s]]
            step3[d]["scales"] = send(picked_s[d], three_s[d], d)

    def send3(s, h):
        for d in range(2):
            step3[d][s, h] = send(picked[d].at[s, h], three[d].at[s, h], d)

    def send4(h):
        for d in range(2):
            if h == 0:
                step3[d]["scales"].wait_recv()
                step4[d]["scales"] = send(three_s[d].at[2], four_s[d].at[0], d)
            step3[d][2, h].wait_recv()
            step4[d][h] = send(three[d].at[2, h], four[d].at[0, h], d)

    each = range(heads)
    first = [send_to(ids, near.at[k], p) for k, p in enumerate(row_peers)]
    code(0)
    for h in each:
        send1(0, h)
    for u in range(1, count):
        code(u)
    for c in first:
        c.wait_recv()
    total = ids[...]
    for k in range(len(row_peers)):
        total = total + near[k]
    tile[0] = total
    first = [send_to(tile.at[0], side.at[k], p) for k, p in enumerate(col_peers)]
    for c in first:
        c.wait_recv()
    for k in range(len(col_peers)):
        total = total + side[k]
    tile[1] = total
    table[0] = total
    first = [send_to(tile.at[1], table.at[k + 1], p) for k, p in enumerate(beam_peers)]
    for d in range(2):
        step1[d]["scales"] = send(qs, one_s[d], d)
    for u in range(1, count - 1):
        for h in each:
            send1(u, h)
    for c in first:
        c.wait_recv()
    to_scalars = pltpu.make_async_copy(table, wants, copied)
    to_scalars.start()
    look_up()
    to_scalars.wait()
    opposite, straight = [], []
    for d in range(2):
        opposite.append(send_to(looked.at[across, halves[d]], opposite_half[d], col_ways[d]))
    for d in range(2):
        straight.append(
            send_to(
                looked.at[cols[d], halves[1 - d]], from_cols[d].at[halves[1 - d]], col_ways[d]
            )
        )
    for d in range(2):
        step1[d]["scales"].wait_recv()
        step2[d]["scales"] = send(one_s[d], two_s[d], d)
    for h in each:
        send1(count - 1, h)
    for h in each:
        send2(0, h)
    todo = [functools.partial(send2, u, h) for u in range(1, count) for h in each]
    todo += [functools.partial(send3, s, h) for s in (2, 0) for h in each]
    picking = todo[len(todo) - 2 * heads]
    todo += [functools.partial(send4, h) for h in each]
    todo += [functools.partial(send3, 1, h) for h in each]
    for d in range(2):
        opposite[d].wait()
        part = part_sum[d]
        add(part, opposite_half[d], looked.at[cols[d], halves[d]])
        straight.append(send_to(part, from_cols[d].at[halves[d]], col_ways[d]))
    for c in straight:
        c.wait_recv()
    add(col_sum, looked.at[col], from_cols[0], from_cols[1])

    reach = (blocks // 2, blocks // 2 - 1)
    passed = [[] for _ in range(2)]

    def block(distance):
        z = (my_beam * rows + row + blocks + distance) % blocks
        return (z % rows) * BEAMS + (my_beam + BEAMS - z // rows) % BEAMS

    def pass_on():
        for d in range(2):
            k = len(passed[d])
            if k == reach[d]:
                continue
            at_block = block(reach[d] - k if d == 0 else k - reach[d])
            if k == 0:
                src = col_sum.at[at_block]
            else:
                passed[d][k - 1].wait_recv()
                hops[d][k] = col_sum[at_block] + from_row[d][k - 1]
                src = hops[d].at[k]
            passed[d].append(send_to(src, from_row[d].at[k], row_ways[d]))

    pass_on()
    for i, unit in enumerate(todo):
        if unit is picking:
            pick()
        unit()
        while len(passed[0]) < min(reach[0], 1 + (i + 1) * reach[0] // len(todo)):
            pass_on()
    for d in range(2):
        passed[d][-1].wait_recv()
    entries[...] = (
        col_sum[block(0)] + from_row[0][reach[0] - 1] + from_row[1][reach[1] - 1]
    ).astype(jnp.float32)
    for d in range(2):
        for key, c in step3[d].items():
            if key != "scales" and key[0] != 2:
                c.wait_recv()
        for c in step4[d].values():
            c.wait_recv()
    mine = wanted_by(0)
    for u in range(count):
        offset = (my_beam + BEAMS - mine(u)) % BEAMS
        third = [jnp.where(lowest(mine, beam(d), count) == u, 0, 1) for d in (-3, 3)]
        middle = lowest(mine, beam(4), count) == u
        rows_out = []
        for h in range(states.shape[1]):
            x = states[u, h]
            line = u * states.shape[1] + h

            def take(x, when, code, scale):
                return jnp.where(when, code.astype(jnp.int32).astype(jnp.float32) * scale, x)

            for d in range(2):
                x = take(
                    x, offset == (1, BEAMS - 1)[d], one[d][u, h], one_s[d][u, h : h + 1, :]
                )
                x = take(
                    x, offset == (2, BEAMS - 2)[d], two[d][u, h], two_s[d][u, h : h + 1, :]
                )
                x = take(
                    x, offset == (3, BEAMS - 3)[d],
                    three[d][third[d], h], three_s[d][third[d], h : h + 1, :],
                )
                x = take(
                    x, (offset == 4) & (middle if d == 0 else jnp.logical_not(middle)),
                    four[d][0, h], four_s[d][0, h : h + 1, :],
                )
            state, out = advance(x, lambda k: entries[line : line + 1, k], gain[h : h + 1, :])
            new_states[u, h] = state
            rows_out.append(out)
        readout[u] = jnp.concatenate(rows_out, axis=0).astype(jnp.bfloat16)
    for c in copies:
        if id(c) not in set(map(id, opposite)):
            c.wait_send()


def step(states, ids, rows_of_tokens, gain):
    count, heads, size, _ = states.shape
    blocks = lax.axis_size("beam") // ROW
    rows = blocks // BEAMS
    height, width = count * heads, rows_of_tokens.shape[1]
    sends = 2 * heads * (2 * count + 4) + 2 * 4 + 6 + blocks - 1 + (rows - 1) + (ROW - 1) + BEAMS - 1
    whole = pl.BlockSpec(memory_space=pltpu.VMEM)
    kept = [count, count, 3, 3, 1, 1, 3, 3]
    parts = [blocks // 2] * 2 + [blocks] * 2 + [blocks // 2] * 6 + [blocks]
    kind = rows_of_tokens.dtype
    codes, floats, block = jnp.int16, jnp.float32, (height, width)
    return pl.pallas_call(
        functools.partial(step_kernel, count),
        out_shape=(
            jax.ShapeDtypeStruct((count, heads, size), jnp.bfloat16),
            jax.ShapeDtypeStruct(states.shape, floats),
        ),
        in_specs=[whole] * 4,
        out_specs=(whole, whole),
        scratch_shapes=[
            *(pltpu.VMEM((k, heads, size, size), codes) for k in kept),
            *(pltpu.VMEM((k, heads, size), floats) for k in kept),
            *(pltpu.VMEM((count, heads, size, size), codes) for _ in range(2)),
            *(pltpu.VMEM((count, heads, size), floats) for _ in range(2)),
            *(pltpu.VMEM((k, *block), kind) for k in parts),
            pltpu.VMEM(block, floats),
            pltpu.VMEM((ROW, blocks, *block), kind),
            pltpu.VMEM((count, heads, size, size), codes),
            pltpu.VMEM((count, heads, size), floats),
            pltpu.VMEM((rows - 1, *ids.shape), jnp.int32),
            pltpu.VMEM((ROW - 1, *ids.shape), jnp.int32),
            pltpu.VMEM((2, *ids.shape), jnp.int32),
            pltpu.VMEM((BEAMS, *ids.shape), jnp.int32),
            pltpu.SMEM((BEAMS, *ids.shape), jnp.int32),
            pltpu.SemaphoreType.DMA,
            pltpu.SemaphoreType.DMA((sends,)),
            pltpu.SemaphoreType.DMA((sends,)),
        ],
        compiler_params=pltpu.CompilerParams(
            collective_id=0, has_side_effects=True, vmem_limit_bytes=48 << 20
        ),
    )(states, ids, rows_of_tokens, gain)


def local(states, parent_beam, next_token, proj_table, gate_table, gain):
    count, heads, size, _ = states.shape
    spacing = lax.axis_size("beam") // BEAMS
    within = lax.axis_index("beam") % spacing
    lanes = 128
    given = jnp.zeros((8 * lanes,), jnp.int32)
    given = lax.dynamic_update_slice(
        given, jnp.repeat(next_token, heads), (within * count * heads,)
    )
    given = lax.dynamic_update_slice(given, parent_beam, (2 * lanes + within * count,))
    vocab_rows = proj_table.shape[0]
    padded = jnp.concatenate(
        [
            proj_table.transpose(1, 0, 2),
            gate_table.transpose(2, 0, 1),
            jnp.zeros((heads, vocab_rows, size - 3), proj_table.dtype),
        ],
        axis=2,
    ).reshape(heads * vocab_rows, 6 * size)
    return step(states, given.reshape(8, lanes), padded, gain)


def solution(mesh):
    return jax.shard_map(
        local,
        mesh=mesh,
        in_specs=(
            P(("groups", "beam"), "mp", None, None),
            P(("groups", "beam")),
            P(("groups", "beam")),
            P("beam", "mp", None),
            P("beam", None, "mp"),
            P("mp", None),
        ),
        out_specs=(P(("groups", "beam"), "mp", None), P(("groups", "beam"), "mp", None, None)),
        check_vma=False,
    )
```

time: 244 us -> 234 us (0.959)
  the two profiles are of different devices: /device:TPU:44 before, /device:TPU:42 now
where the time goes in v5:
time: 234 us; the launch traced here: 233 us
  Pallas kernels  226 us (97%)
  local copies, waits for them, and re-layouts  5.52 us (2%)
    pallas_call x1, Pallas kernels, step(): pl.pallas_call(functools.partial(step_kernel, count), out_shape=(jax.Shap...  226 us

profile of v5, /device:TPU:42, one launch (start us, length us, event | category | flops | bytes accessed | tf_op | source)
XLA Modules:
  0.0 233.4 jit_solution(394856898593925305)
XLA Ops:
  0.7 0.1 pad.2.clone
  0.7 0.7 broadcast_in_dim.10
  1.5 0.1 reshape.13
  1.6 0.2 dynamic_update_slice.6
  1.7 0.8 dynamic_update_slice.7
  2.6 0.9 copy.8
  3.4 1.5 maximum_maximum_fusion
  5.0 0.0 copy-start
  5.0 0.0 copy-start.1
  5.0 0.1 copy.9
  5.1 1.1 copy-done
  6.2 0.0 copy-done.1
  6.2 225.7 %shard_map.77 = (bf16[4,4,128]{2,1,0:T(4,128)(2,1)S(1)}, f32[4,4,128,128]{3,2,1,0:T(8,128)S(1)}) custom-call(f32[4,4,128,128]{3,2,1,0:T(8,128)S(1)} %copy-done, s32[8,128]{1,0:T(8,128)S(1)} %bitcast.5, bf16[512,768]{1,0:T(8,128)(2,1)S(1)} %bitcast.4, f32[4,128]{1,0:T(4,128)S(1)} %copy-done.1), custom_call_target="tpu_custom_call" | custom-call | tf_op jit(solution)/shard_map/pallas_call | solution.py:352
  231.9 0.6 copy.14
  232.4 1.0 copy.15
  (2 shorter events, 0.0 us)
Async XLA Ops:
  5.0 1.2 copy-start
  5.0 1.2 copy-start.1

commit v6 on v5

--- a/solution.py
+++ b/solution.py
@@ -60,12 +60,16 @@
 
 
 def step_kernel(count, states, ids, rows_of_tokens, gain, readout, new_states, *scratch):
-    two, three, four, picked = scratch[0:2], scratch[2:4], scratch[4:6], scratch[6:8]
-    two_s, three_s, four_s, picked_s = scratch[8:10], scratch[10:12], scratch[12:14], scratch[14:16]
-    one, one_s = scratch[16:18], scratch[18:20]
-    opposite_half, from_cols, part_sum = scratch[20:22], scratch[22:24], scratch[24:26]
-    hops, from_row = scratch[26:28], scratch[28:30]
-    col_sum, entries, looked, q, qs, near, side, tile, table, wants, copied, sems, rsem = scratch[30:]
+    heads = states.shape[1]
+    refs = iter(scratch)
+
+    def take_refs(k):
+        return [next(refs) for _ in range(k)]
+
+    two, three, four, picked = ([take_refs(heads) for _ in range(2)] for _ in range(4))
+    two_s, three_s, four_s, picked_s, one, one_s = (take_refs(2) for _ in range(6))
+    opposite_half, from_cols, part_sum, hops, from_row = (take_refs(2) for _ in range(5))
+    col_sum, entries, looked, q, qs, near, side, tile, table, wants, copied, sems, rsem = refs
     n = lax.axis_size("beam")
     me = lax.axis_index("beam")
     spacing = n // BEAMS
@@ -123,8 +127,8 @@
     half = blocks // 2
     halves = (pl.ds(0, half), pl.ds(half, half))
 
-    def code(u):
-        for h in range(states.shape[1]):
+    def code(h):
+        for u in range(count):
             x = states[u, h]
             top = jnp.maximum(jnp.max(jnp.abs(x), axis=0, keepdims=True), 1e-30)
             qs[u, h : h + 1, :] = top * (1.0 / LEVELS)
@@ -134,7 +138,6 @@
 
     def look_up():
         lines = rows_of_tokens.shape[0]
-        heads = states.shape[1]
         vocab_rows = lines // heads
         lanes = tile.shape[-1]
         per = count * heads
@@ -154,7 +157,6 @@
                     dev = r * (lanes // per) + w
                     looked[dev % ROW, (dev // ROW) * BEAMS + k] = out[w * per : (w + 1) * per, :]
 
-    heads = states.shape[1]
     step1 = [{}, {}]
     step2 = [{}, {}]
     step3 = [{}, {}]
@@ -167,30 +169,36 @@
     def send2(u, h):
         for d in range(2):
             step1[d][u, h].wait_recv()
-            step2[d][u, h] = send(one[d].at[u, h], two[d].at[u, h], d)
-
-    def pick():
-        for d in range(2):
-            for c in step2[d].values():
-                c.wait_recv()
-            sign = 1 if d == 0 else -1
-            origin = beam(-2 * sign)
-            nearer = wanted_by(sign)
-            farther = wanted_by(2 * sign)
-            end = lowest if d == 0 else highest
-            chosen = (
-                lowest(nearer, origin, count),
-                highest(nearer, origin, count),
-                end(farther, origin, count),
-            )
-            for s in (2, 0, 1):
-                picked_s[d][s] = two_s[d][chosen[s]]
-                picked[d][s] = two[d][chosen[s]]
-            step3[d]["scales"] = send(picked_s[d], three_s[d], d)
-
-    def send3(s, h):
-        for d in range(2):
-            step3[d][s, h] = send(picked[d].at[s, h], three[d].at[s, h], d)
+            step2[d][u, h] = send(one[d].at[u, h], two[d][h].at[u], d)
+
+    def choice(d):
+        sign = 1 if d == 0 else -1
+        origin = beam(-2 * sign)
+        nearer = wanted_by(sign)
+        end = lowest if d == 0 else highest
+        return (
+            lowest(nearer, origin, count),
+            highest(nearer, origin, count),
+            end(wanted_by(2 * sign), origin, count),
+        )
+
+    def pick(h, chosen):
+        for d in range(2):
+            if h == 0:
+                step2[d]["scales"].wait_recv()
+                for s in range(3):
+                    picked_s[d][s] = two_s[d][chosen[d][s]]
+                step3[d]["scales"] = send(picked_s[d], three_s[d], d)
+            for u in range(count):
+                step2[d][u, h].wait_recv()
+            for s in range(3):
+                picked[d][h][s] = two[d][h][chosen[d][s]]
+
+    def send3(s, h, chosen):
+        if s == 2:
+            pick(h, chosen)
+        for d in range(2):
+            step3[d][s, h] = send(picked[d][h].at[s], three[d][h].at[s], d)
 
     def send4(h):
         for d in range(2):
@@ -198,15 +206,16 @@
                 step3[d]["scales"].wait_recv()
                 step4[d]["scales"] = send(three_s[d].at[2], four_s[d].at[0], d)
             step3[d][2, h].wait_recv()
-            step4[d][h] = send(three[d].at[2, h], four[d].at[0, h], d)
+            step4[d][h] = send(three[d][h].at[2], four[d][h].at[0], d)
 
     each = range(heads)
     first = [send_to(ids, near.at[k], p) for k, p in enumerate(row_peers)]
+    every = range(count)
     code(0)
-    for h in each:
-        send1(0, h)
-    for u in range(1, count):
-        code(u)
+    for u in every:
+        send1(u, 0)
+    for h in each[1:]:
+        code(h)
     for c in first:
         c.wait_recv()
     total = ids[...]
@@ -223,8 +232,8 @@
     first = [send_to(tile.at[1], table.at[k + 1], p) for k, p in enumerate(beam_peers)]
     for d in range(2):
         step1[d]["scales"] = send(qs, one_s[d], d)
-    for u in range(1, count - 1):
-        for h in each:
+    for h in each[1:-1]:
+        for u in every:
             send1(u, h)
     for c in first:
         c.wait_recv()
@@ -244,15 +253,20 @@
     for d in range(2):
         step1[d]["scales"].wait_recv()
         step2[d]["scales"] = send(one_s[d], two_s[d], d)
+    for u in every:
+        send1(u, heads - 1)
+    for u in every:
+        send2(u, 0)
+    todo = [functools.partial(send2, u, h) for h in each[1:] for u in every]
+    chosen = [choice(d) for d in range(2)]
     for h in each:
-        send1(count - 1, h)
-    for h in each:
-        send2(0, h)
-    todo = [functools.partial(send2, u, h) for u in range(1, count) for h in each]
-    todo += [functools.partial(send3, s, h) for s in (2, 0) for h in each]
-    picking = todo[len(todo) - 2 * heads]
-    todo += [functools.partial(send4, h) for h in each]
-    todo += [functools.partial(send3, 1, h) for h in each]
+        todo.append(functools.partial(send3, 2, h, chosen))
+        if h > 0:
+            todo.append(functools.partial(send4, h - 1))
+        todo.append(functools.partial(send3, 0, h, chosen))
+        if h == heads - 1:
+            todo.append(functools.partial(send4, h))
+        todo.append(functools.partial(send3, 1, h, chosen))
     for d in range(2):
         opposite[d].wait()
         part = part_sum[d]
@@ -285,8 +299,6 @@
 
     pass_on()
     for i, unit in enumerate(todo):
-        if unit is picking:
-            pick()
         unit()
         while len(passed[0]) < min(reach[0], 1 + (i + 1) * reach[0] // len(todo)):
             pass_on()
@@ -296,43 +308,41 @@
         col_sum[block(0)] + from_row[0][reach[0] - 1] + from_row[1][reach[1] - 1]
     ).astype(jnp.float32)
     for d in range(2):
-        for key, c in step3[d].items():
-            if key != "scales" and key[0] != 2:
-                c.wait_recv()
-        for c in step4[d].values():
-            c.wait_recv()
+        step4[d]["scales"].wait_recv()
     mine = wanted_by(0)
-    for u in range(count):
-        offset = (my_beam + BEAMS - mine(u)) % BEAMS
-        third = [jnp.where(lowest(mine, beam(d), count) == u, 0, 1) for d in (-3, 3)]
-        middle = lowest(mine, beam(4), count) == u
-        rows_out = []
-        for h in range(states.shape[1]):
+    offsets = [(my_beam + BEAMS - mine(u)) % BEAMS for u in every]
+    third = [[jnp.where(lowest(mine, beam(b), count) == u, 0, 1) for b in (-3, 3)] for u in every]
+    across_first = lowest(mine, beam(4), count)
+
+    def take(x, when, code, scale):
+        return jnp.where(when, code.astype(jnp.int32).astype(jnp.float32) * scale, x)
+
+    outs = [[] for _ in every]
+    for h in each:
+        for d in range(2):
+            step3[d][0, h].wait_recv()
+            step3[d][1, h].wait_recv()
+            step4[d][h].wait_recv()
+        at_h = slice(h, h + 1)
+        for u in every:
             x = states[u, h]
-            line = u * states.shape[1] + h
-
-            def take(x, when, code, scale):
-                return jnp.where(when, code.astype(jnp.int32).astype(jnp.float32) * scale, x)
-
+            offset = offsets[u]
+            middle = across_first == u
             for d in range(2):
-                x = take(
-                    x, offset == (1, BEAMS - 1)[d], one[d][u, h], one_s[d][u, h : h + 1, :]
-                )
-                x = take(
-                    x, offset == (2, BEAMS - 2)[d], two[d][u, h], two_s[d][u, h : h + 1, :]
-                )
-                x = take(
-                    x, offset == (3, BEAMS - 3)[d],
-                    three[d][third[d], h], three_s[d][third[d], h : h + 1, :],
-                )
+                t = third[u][d]
+                x = take(x, offset == (1, BEAMS - 1)[d], one[d][u, h], one_s[d][u, at_h, :])
+                x = take(x, offset == (2, BEAMS - 2)[d], two[d][h][u], two_s[d][u, at_h, :])
+                x = take(x, offset == (3, BEAMS - 3)[d], three[d][h][t], three_s[d][t, at_h, :])
                 x = take(
                     x, (offset == 4) & (middle if d == 0 else jnp.logical_not(middle)),
-                    four[d][0, h], four_s[d][0, h : h + 1, :],
+                    four[d][h][0], four_s[d][0, at_h, :],
                 )
-            state, out = advance(x, lambda k: entries[line : line + 1, k], gain[h : h + 1, :])
+            line = u * heads + h
+            state, out = advance(x, lambda k: entries[line : line + 1, k], gain[at_h, :])
             new_states[u, h] = state
-            rows_out.append(out)
-        readout[u] = jnp.concatenate(rows_out, axis=0).astype(jnp.bfloat16)
+            outs[u].append(out)
+    for u in every:
+        readout[u] = jnp.concatenate(outs[u], axis=0).astype(jnp.bfloat16)
     for c in copies:
         if id(c) not in set(map(id, opposite)):
             c.wait_send()
@@ -358,7 +368,7 @@
         in_specs=[whole] * 4,
         out_specs=(whole, whole),
         scratch_shapes=[
-            *(pltpu.VMEM((k, heads, size, size), codes) for k in kept),
+            *(pltpu.VMEM((k, size, size), codes) for k in kept for _ in range(heads)),
             *(pltpu.VMEM((k, heads, size), floats) for k in kept),
             *(pltpu.VMEM((count, heads, size, size), codes) for _ in range(2)),
             *(pltpu.VMEM((count, heads, size), floats) for _ in range(2)),

time: 234 us -> 231 us (0.987)
  Pallas kernels: 226 us -> 223 us
    pallas_call x1, Pallas kernels: 226 us -> 223 us  [step(): pl.pallas_call(functools.partial(step_kernel, count), out_shape=(jax.Shap...]
where the time goes in v6:
time: 231 us; the launch traced here: 230 us
  Pallas kernels  223 us (97%)
  local copies, waits for them, and re-layouts  5.52 us (2%)
    pallas_call x1, Pallas kernels, step(): pl.pallas_call(functools.partial(step_kernel, count), out_shape=(jax.Shap...  223 us

profile of v6, /device:TPU:42, one launch (start us, length us, event | category | flops | bytes accessed | tf_op | source)
XLA Modules:
  0.0 230.4 jit_solution(3053855408744667024)
XLA Ops:
  0.7 0.1 pad.2.clone
  0.7 0.7 broadcast_in_dim.10
  1.5 0.1 reshape.13
  1.6 0.2 dynamic_update_slice.6
  1.7 0.8 dynamic_update_slice.7
  2.6 0.9 copy.8
  3.4 1.5 maximum_maximum_fusion
  5.0 0.0 copy-start
  5.0 0.0 copy-start.1
  5.0 0.1 copy.9
  5.1 1.1 copy-done
  6.2 0.0 copy-done.1
  6.2 222.6 %shard_map.77 = (bf16[4,4,128]{2,1,0:T(4,128)(2,1)S(1)}, f32[4,4,128,128]{3,2,1,0:T(8,128)S(1)}) custom-call(f32[4,4,128,128]{3,2,1,0:T(8,128)S(1)} %copy-done, s32[8,128]{1,0:T(8,128)S(1)} %bitcast.5, bf16[512,768]{1,0:T(8,128)(2,1)S(1)} %bitcast.4, f32[4,128]{1,0:T(4,128)S(1)} %copy-done.1), custom_call_target="tpu_custom_call" | custom-call | tf_op jit(solution)/shard_map/pallas_call | solution.py:362
  228.8 0.6 copy.14
  229.4 1.0 copy.15
  (2 shorter events, 0.0 us)
Async XLA Ops:
  5.0 1.2 copy-start
  5.0 1.2 copy-start.1

commit v7 on v6

--- a/solution.py
+++ b/solution.py
@@ -59,8 +59,10 @@
     return state, gain * row * scale
 
 
-def step_kernel(count, states, ids, rows_of_tokens, gain, readout, new_states, *scratch):
-    heads = states.shape[1]
+def step_kernel(
+    count, tokens, parents, states_in, rows_of_tokens, gain, readout, new_states, *scratch
+):
+    heads, size = states_in.shape[1], states_in.shape[2]
     refs = iter(scratch)
 
     def take_refs(k):
@@ -69,7 +71,10 @@
     two, three, four, picked = ([take_refs(heads) for _ in range(2)] for _ in range(4))
     two_s, three_s, four_s, picked_s, one, one_s = (take_refs(2) for _ in range(6))
     opposite_half, from_cols, part_sum, hops, from_row = (take_refs(2) for _ in range(5))
-    col_sum, entries, looked, q, qs, near, side, tile, table, wants, copied, sems, rsem = refs
+    col_sum, entries, looked, states, q, qs, ids, near, side, tile, table, wants = take_refs(12)
+    copied, fetched, ready, sems, rsem = refs
+    fetch = pltpu.make_async_copy(states_in, states, fetched)
+    fetch.start()
     n = lax.axis_size("beam")
     me = lax.axis_index("beam")
     spacing = n // BEAMS
@@ -87,7 +92,7 @@
     beam_peers = [(me + k * spacing) % n for k in range(1, BEAMS)]
     row_peers = [base + ((row + k) % rows) * ROW + col for k in range(1, rows)]
     col_peers = [base + row * ROW + (col + k) % ROW for k in range(1, ROW)]
-    peers = [*beam_peers, *row_peers, *col_peers, *row_ways]
+    peers = [*ways, *row_peers, *col_peers, *row_ways]
     for p in peers:
         pl.semaphore_signal(barrier, inc=1, **to(p))
     pl.semaphore_wait(barrier, len(peers))
@@ -209,11 +214,32 @@
             step4[d][h] = send(three[d][h].at[2], four[d][h].at[0], d)
 
     each = range(heads)
+    def announce(j):
+        for d in range(2):
+            pl.semaphore_signal(ready.at[d, j], inc=1, **to(ways[d]))
+
+    def hear(j):
+        for d in range(2):
+            pl.semaphore_wait(ready.at[d, j], 1)
+
+    lanes = ids.shape[1]
+    spot = lax.broadcasted_iota(jnp.int32, ids.shape, 0) * lanes
+    spot = spot + lax.broadcasted_iota(jnp.int32, ids.shape, 1)
+    own = jnp.zeros(ids.shape, jnp.int32)
+    for u in range(count):
+        start = (within * count + u) * heads
+        own = jnp.where((spot >= start) & (spot < start + heads), tokens[u], own)
+        own = jnp.where(spot == 2 * lanes + within * count + u, parents[u], own)
+    ids[...] = own
+    every = range(count)
+    announce(0)
     first = [send_to(ids, near.at[k], p) for k, p in enumerate(row_peers)]
-    every = range(count)
+    fetch.wait()
     code(0)
     for u in every:
         send1(u, 0)
+    hear(0)
+    announce(1)
     for h in each[1:]:
         code(h)
     for c in first:
@@ -223,12 +249,15 @@
         total = total + near[k]
     tile[0] = total
     first = [send_to(tile.at[0], side.at[k], p) for k, p in enumerate(col_peers)]
+    hear(1)
+    announce(2)
     for c in first:
         c.wait_recv()
     for k in range(len(col_peers)):
         total = total + side[k]
     tile[1] = total
     table[0] = total
+    hear(2)
     first = [send_to(tile.at[1], table.at[k + 1], p) for k, p in enumerate(beam_peers)]
     for d in range(2):
         step1[d]["scales"] = send(qs, one_s[d], d)
@@ -348,7 +377,7 @@
             c.wait_send()
 
 
-def step(states, ids, rows_of_tokens, gain):
+def step(tokens, parents, states, rows_of_tokens, gain):
     count, heads, size, _ = states.shape
     blocks = lax.axis_size("beam") // ROW
     rows = blocks // BEAMS
@@ -358,14 +387,15 @@
     kept = [count, count, 3, 3, 1, 1, 3, 3]
     parts = [blocks // 2] * 2 + [blocks] * 2 + [blocks // 2] * 6 + [blocks]
     kind = rows_of_tokens.dtype
-    codes, floats, block = jnp.int16, jnp.float32, (height, width)
+    codes, floats, block, ids = jnp.int16, jnp.float32, (height, width), (8, 128)
+    scalars = pl.BlockSpec(memory_space=pltpu.SMEM)
     return pl.pallas_call(
         functools.partial(step_kernel, count),
         out_shape=(
             jax.ShapeDtypeStruct((count, heads, size), jnp.bfloat16),
             jax.ShapeDtypeStruct(states.shape, floats),
         ),
-        in_specs=[whole] * 4,
+        in_specs=[scalars, scalars, pl.BlockSpec(memory_space=pltpu.HBM), whole, whole],
         out_specs=(whole, whole),
         scratch_shapes=[
             *(pltpu.VMEM((k, size, size), codes) for k in kept for _ in range(heads)),
@@ -375,33 +405,29 @@
             *(pltpu.VMEM((k, *block), kind) for k in parts),
             pltpu.VMEM(block, floats),
             pltpu.VMEM((ROW, blocks, *block), kind),
-            pltpu.VMEM((count, heads, size, size), codes),
+            pltpu.VMEM(states.shape, floats),
+            pltpu.VMEM(states.shape, codes),
             pltpu.VMEM((count, heads, size), floats),
-            pltpu.VMEM((rows - 1, *ids.shape), jnp.int32),
-            pltpu.VMEM((ROW - 1, *ids.shape), jnp.int32),
-            pltpu.VMEM((2, *ids.shape), jnp.int32),
-            pltpu.VMEM((BEAMS, *ids.shape), jnp.int32),
-            pltpu.SMEM((BEAMS, *ids.shape), jnp.int32),
+            pltpu.VMEM(ids, jnp.int32),
+            pltpu.VMEM((rows - 1, *ids), jnp.int32),
+            pltpu.VMEM((ROW - 1, *ids), jnp.int32),
+            pltpu.VMEM((2, *ids), jnp.int32),
+            pltpu.VMEM((BEAMS, *ids), jnp.int32),
+            pltpu.SMEM((BEAMS, *ids), jnp.int32),
             pltpu.SemaphoreType.DMA,
+            pltpu.SemaphoreType.DMA,
+            pltpu.SemaphoreType.REGULAR((2, BEAMS // 2 - 1)),
             pltpu.SemaphoreType.DMA((sends,)),
             pltpu.SemaphoreType.DMA((sends,)),
         ],
         compiler_params=pltpu.CompilerParams(
             collective_id=0, has_side_effects=True, vmem_limit_bytes=48 << 20
         ),
-    )(states, ids, rows_of_tokens, gain)
+    )(tokens, parents, states, rows_of_tokens, gain)
 
 
 def local(states, parent_beam, next_token, proj_table, gate_table, gain):
-    count, heads, size, _ = states.shape
-    spacing = lax.axis_size("beam") // BEAMS
-    within = lax.axis_index("beam") % spacing
-    lanes = 128
-    given = jnp.zeros((8 * lanes,), jnp.int32)
-    given = lax.dynamic_update_slice(
-        given, jnp.repeat(next_token, heads), (within * count * heads,)
-    )
-    given = lax.dynamic_update_slice(given, parent_beam, (2 * lanes + within * count,))
+    heads, size = states.shape[1:3]
     vocab_rows = proj_table.shape[0]
     padded = jnp.concatenate(
         [
@@ -411,7 +437,7 @@
         ],
         axis=2,
     ).reshape(heads * vocab_rows, 6 * size)
-    return step(states, given.reshape(8, lanes), padded, gain)
+    return step(next_token, parent_beam, states, padded, gain)
 
 
 def solution(mesh):

time: 231 us -> 231 us (level)
  the two profiles are of different devices: /device:TPU:42 before, /device:TPU:40 now
where the time goes in v7:
time: 231 us
  Pallas kernels  225 us (97%)
  local copies, waits for them, and re-layouts  3.7 us (2%)
    pallas_call x1, Pallas kernels, step(): pl.pallas_call(functools.partial(step_kernel, count), out_shape=(jax.Shap...  225 us

profile of v7, /device:TPU:40, one launch (start us, length us, event | category | flops | bytes accessed | tf_op | source)
XLA Modules:
  0.0 230.5 jit_solution(14385341704748131218)
XLA Ops:
  0.6 0.1 pad.2.clone
  0.7 0.9 copy.8
  1.6 1.5 maximum_maximum_fusion
  3.1 0.0 copy-start
  3.1 0.0 copy-start.1
  3.1 0.0 copy-start.2
  3.2 0.0 copy-start.3
  3.2 0.1 copy.9
  3.3 1.1 copy-done
  4.3 0.0 copy-done.1
  4.3 0.0 copy-done.2
  4.4 0.0 copy-done.3
  4.4 224.6 %shard_map.77 = (bf16[4,4,128]{2,1,0:T(4,128)(2,1)S(1)}, f32[4,4,128,128]{3,2,1,0:T(8,128)S(1)}) custom-call(s32[4]{0:T(128)S(1)} %copy-done.2, s32[4]{0:T(128)S(1)} %copy-done.3, f32[4,4,128,128]{3,2,1,0:T(8,128)S(1)} %copy-done, bf16[512,768]{1,0:T(8,128)(2,1)S(1)} %bitcast.3, f32[4,128]{1,0:T(4,128)S(1)} %copy-done.1), custom_call_target="tpu_custom_call" | custom-call | tf_op jit(solution)/shard_map/pallas_call | solution.py:392
  229.0 0.6 copy.12
  229.6 1.0 copy.13
  (1 shorter events, 0.0 us)
Async XLA Ops:
  3.1 1.2 copy-start
  3.1 1.2 copy-start.1
  3.1 1.2 copy-start.2
  3.2 1.2 copy-start.3

commit v8 on v7

--- a/solution.py
+++ b/solution.py
@@ -70,7 +70,8 @@
 
     two, three, four, picked = ([take_refs(heads) for _ in range(2)] for _ in range(4))
     two_s, three_s, four_s, picked_s, one, one_s = (take_refs(2) for _ in range(6))
-    opposite_half, from_cols, part_sum, hops, from_row = (take_refs(2) for _ in range(5))
+    opposite_half, from_cols, part_sum, hops, from_row, from_pair = (take_refs(2) for _ in range(6))
+    pair_sum = next(refs)
     col_sum, entries, looked, states, q, qs, ids, near, side, tile, table, wants = take_refs(12)
     copied, fetched, ready, sems, rsem = refs
     fetch = pltpu.make_async_copy(states_in, states, fetched)
@@ -87,7 +88,9 @@
     cols = ((col + 1) % ROW, (col + ROW - 1) % ROW)
     across = (col + 2) % ROW
     col_ways = [base + row * ROW + c for c in cols]
-    row_ways = ((me + ROW) % n, (me + n - ROW) % n)
+    row_ways = ((me + 2 * ROW) % n, (me + n - 2 * ROW) % n)
+    parity = row % 2
+    partner = base + (row + 1 - 2 * parity) * ROW + col
     barrier = pltpu.get_barrier_semaphore()
     beam_peers = [(me + k * spacing) % n for k in range(1, BEAMS)]
     row_peers = [base + ((row + k) % rows) * ROW + col for k in range(1, rows)]
@@ -301,16 +304,37 @@
         part = part_sum[d]
         add(part, opposite_half[d], looked.at[cols[d], halves[d]])
         straight.append(send_to(part, from_cols[d].at[halves[d]], col_ways[d]))
+    for unit in todo[:count]:
+        unit()
     for c in straight:
         c.wait_recv()
     add(col_sum, looked.at[col], from_cols[0], from_cols[1])
 
-    reach = (blocks // 2, blocks // 2 - 1)
+    swaps = [
+        send_to(
+            col_sum.at[pl.ds((1 - parity + 2 * i) * BEAMS, BEAMS)],
+            from_pair[i], partner,
+        )
+        for i in range(2)
+    ]
+    for unit in todo[count : 2 * count]:
+        unit()
+    todo = todo[2 * count :]
+    for c in swaps:
+        c.wait_recv()
+
+    def pair(k, _):
+        for i in range(2):
+            pair_sum[i * BEAMS + k] = col_sum[(parity + 2 * i) * BEAMS + k] + from_pair[i][k]
+        return 0
+
+    lax.fori_loop(0, BEAMS, pair, 0)
+    reach = (blocks // 4, blocks // 4 - 1)
     passed = [[] for _ in range(2)]
 
     def block(distance):
-        z = (my_beam * rows + row + blocks + distance) % blocks
-        return (z % rows) * BEAMS + (my_beam + BEAMS - z // rows) % BEAMS
+        z = (my_beam * rows + row + 2 * blocks + 2 * distance) % blocks
+        return (z % rows) // 2 * BEAMS + (my_beam + BEAMS - z // rows) % BEAMS
 
     def pass_on():
         for d in range(2):
@@ -319,10 +343,10 @@
                 continue
             at_block = block(reach[d] - k if d == 0 else k - reach[d])
             if k == 0:
-                src = col_sum.at[at_block]
+                src = pair_sum.at[at_block]
             else:
                 passed[d][k - 1].wait_recv()
-                hops[d][k] = col_sum[at_block] + from_row[d][k - 1]
+                hops[d][k] = pair_sum[at_block] + from_row[d][k - 1]
                 src = hops[d].at[k]
             passed[d].append(send_to(src, from_row[d].at[k], row_ways[d]))
 
@@ -334,7 +358,7 @@
     for d in range(2):
         passed[d][-1].wait_recv()
     entries[...] = (
-        col_sum[block(0)] + from_row[0][reach[0] - 1] + from_row[1][reach[1] - 1]
+        pair_sum[block(0)] + from_row[0][reach[0] - 1] + from_row[1][reach[1] - 1]
     ).astype(jnp.float32)
     for d in range(2):
         step4[d]["scales"].wait_recv()
@@ -382,10 +406,11 @@
     blocks = lax.axis_size("beam") // ROW
     rows = blocks // BEAMS
     height, width = count * heads, rows_of_tokens.shape[1]
-    sends = 2 * heads * (2 * count + 4) + 2 * 4 + 6 + blocks - 1 + (rows - 1) + (ROW - 1) + BEAMS - 1
+    sends = 2 * heads * (2 * count + 4) + 2 * 4 + 6 + 2 + blocks // 2 - 1 + (rows - 1) + (ROW - 1) + BEAMS - 1
     whole = pl.BlockSpec(memory_space=pltpu.VMEM)
     kept = [count, count, 3, 3, 1, 1, 3, 3]
-    parts = [blocks // 2] * 2 + [blocks] * 2 + [blocks // 2] * 6 + [blocks]
+    parts = [blocks // 2] * 2 + [blocks] * 2 + [blocks // 2] * 2 + [blocks // 4] * 4
+    parts += [BEAMS] * 2 + [2 * BEAMS, blocks]
     kind = rows_of_tokens.dtype
     codes, floats, block, ids = jnp.int16, jnp.float32, (height, width), (8, 128)
     scalars = pl.BlockSpec(memory_space=pltpu.SMEM)

time: 231 us -> 218 us (0.944)
  Pallas kernels: 225 us -> 210 us
    pallas_call x1, Pallas kernels: 225 us -> 210 us  [step(): pl.pallas_call(functools.partial(step_kernel, count), out_shape=(jax.Shap...]
where the time goes in v8:
time: 218 us; the launch traced here: 216 us
  Pallas kernels  210 us (96%)
  local copies, waits for them, and re-layouts  3.7 us (2%)
    pallas_call x1, Pallas kernels, step(): pl.pallas_call(functools.partial(step_kernel, count), out_shape=(jax.Shap...  210 us

profile of v8, /device:TPU:40, one launch (start us, length us, event | category | flops | bytes accessed | tf_op | source)
XLA Modules:
  0.0 215.8 jit_solution(8746344862801180279)
XLA Ops:
  0.6 0.1 pad.2.clone
  0.7 0.9 copy.8
  1.6 1.5 maximum_maximum_fusion
  3.1 0.0 copy-start
  3.1 0.0 copy-start.1
  3.1 0.0 copy-start.2
  3.2 0.0 copy-start.3
  3.2 0.1 copy.9
  3.3 1.1 copy-done
  4.3 0.0 copy-done.1
  4.3 0.0 copy-done.2
  4.4 0.0 copy-done.3
  4.4 209.9 %shard_map.77 = (bf16[4,4,128]{2,1,0:T(4,128)(2,1)S(1)}, f32[4,4,128,128]{3,2,1,0:T(8,128)S(1)}) custom-call(s32[4]{0:T(128)S(1)} %copy-done.2, s32[4]{0:T(128)S(1)} %copy-done.3, f32[4,4,128,128]{3,2,1,0:T(8,128)S(1)} %copy-done, bf16[512,768]{1,0:T(8,128)(2,1)S(1)} %bitcast.3, f32[4,128]{1,0:T(4,128)S(1)} %copy-done.1), custom_call_target="tpu_custom_call" | custom-call | tf_op jit(solution)/shard_map/pallas_call | solution.py:417
  214.2 0.6 copy.12
  214.8 1.0 copy.13
  (1 shorter events, 0.0 us)
Async XLA Ops:
  3.1 1.2 copy-start
  3.1 1.2 copy-start.1
  3.1 1.2 copy-start.2
  3.2 1.2 copy-start.3
